TPU v7x, 32 devices: a whole 2x2x4 slice. The times are simulated.
32 devices in a mesh: shard: 16 (over z, x, core), task: 2 (over y).
Axes of the slice: x: 2, y: 2, z: 4, core: 2. Of those that a mesh axis runs over, the one named last changes fastest.
Arguments:
- task_deltas: bfloat16 [2, 4, 256, 16384], P('task', None, 'shard')
- rank_scores: int32 [2, 4, 256, 16384], P('task', None, 'shard'), may hold values from 0 to 1073741823
- keep_limits: int32 [2, 4, 8], P('task'), may hold values from 268435456 to 805306367
Outputs:
- merged: bfloat16 [4, 256, 16384], P(None, 'shard', 'task')
All inputs are finite; a program needn't handle non-finite values.
Results may differ from a plain program's by a relative error of at most 0.0051.
Values may be sent and summed in bfloat16 or wider, within the bound.
A program may use at most 64 MiB of HBM per device.

v0:
```python
import functools
import jax
import jax.numpy as jnp
from jax import lax
from jax.experimental import pallas as pl
from jax.experimental.pallas import tpu as pltpu
from jax.sharding import PartitionSpec as P

EXPERTS = 8
F32 = jnp.float32
MESH = pl.DeviceIdType.MESH


def kernel(
    sizes, delta_hbm, score_hbm, limit_hbm, merged,
    limit_ref, delta, score, outgoing, incoming, sums, sums_in, part, part_in,
    chance, chance_in, own_rate, in_rate, own_kept,
    limit_sem, load_sem, send_sem, recv_sem, sums_sem, part_sem, chance_sem, share_sem,
):
    layers, rows, width, tasks, shards = sizes
    columns = width // tasks
    piece = min(4096, columns)
    pieces = columns // piece
    groups = shards // EXPERTS
    group_bits = groups.bit_length() - 1
    all_bits = shards.bit_length() - 1
    me_shard, me_task = lax.axis_index("shard"), lax.axis_index("task")
    expert = me_shard // groups
    row_total = rows * groups

    def flipped(index, mask):
        for bit in range(all_bits):
            stride = 2**bit
            if mask & stride:
                index = index + stride * (1 - 2 * lax.rem(index // stride, 2))
        return index

    def xor_peer(bit):
        return flipped(me_shard, 2**bit)

    def task_peer(k):
        return lax.rem(me_task + k, tasks)

    limit_copy = pltpu.make_async_copy(limit_hbm.at[0], limit_ref, limit_sem)
    limit_copy.start()
    barrier = pltpu.get_barrier_semaphore()
    for k in range(1, tasks):
        pl.semaphore_signal(barrier, inc=1, device_id={"task": task_peer(k)}, device_id_type=MESH)
    greeted = list(range(1, groups)) + [2**bit for bit in range(group_bits, all_bits)]
    for mask in greeted:
        pl.semaphore_signal(
            barrier, inc=1, device_id={"shard": flipped(me_shard, mask)}, device_id_type=MESH
        )

    loads = {}

    def start_load(l, k):
        cuts = pieces if l == 0 and k else 1
        length = columns // cuts
        for i in range(cuts):
            here = pl.ds(i * length, length)
            there = pl.ds(pl.multiple_of(task_peer(k) * columns + i * length, 128), length)
            loads[l, k, i] = [
                pltpu.make_async_copy(whole.at[0, l, :, there], held.at[l, k, :, here], load_sem.at[l, k, i, j])
                for j, (whole, held) in enumerate(((score_hbm, score), (delta_hbm, delta)))
            ]
            for copy in loads[l, k, i]:
                copy.start()

    def wait_load(l, k, i):
        for copy in loads.get((l, k, i), ()):
            copy.wait()

    for l in range(layers):
        for k in range(1, tasks):
            start_load(l, k)
    limit_copy.wait()

    def at_piece(i):
        return pl.ds(i * piece if isinstance(i, int) else pl.multiple_of(i * piece, 128), piece)

    def masked(l, k, at):
        limit = limit_ref[l, expert]
        return jnp.where(score[l, k, :, at] < limit, delta[l, k, :, at].astype(F32), 0.0)

    sends = {}

    def start_send(l, k, i):
        at = at_piece(i)
        copy = pltpu.make_async_remote_copy(
            src_ref=outgoing.at[l, k - 1, :, at],
            dst_ref=incoming.at[l, k - 1, :, at],
            send_sem=send_sem.at[l, k - 1, i],
            recv_sem=recv_sem.at[l, k - 1, i],
            device_id={"task": task_peer(k)},
            device_id_type=MESH,
        )
        copy.start()
        sends[l, k, i] = copy

    ready = []
    entered = False
    for l in range(layers):
        for k in range(1, tasks):
            for i in range(pieces):
                wait_load(l, k, i)
                at = at_piece(i)
                outgoing[l, k - 1, :, at] = masked(l, k, at).astype(jnp.bfloat16)
                if not entered and ready:
                    pl.semaphore_wait(barrier, tasks - 1 + len(greeted))
                    entered = True
                    owed = True
                if ready and ready[0][0] < layers - 1:
                    start_send(*ready.pop(0))
                    if owed:
                        owed = False
                        for own in range(layers):
                            start_load(own, 0)
                ready.append((l, k, i))

    for k in range(tasks):
        for l in range(layers):
            if k == 0:
                wait_load(l, 0, 0)

            def add_up(i, carry, k=k, l=l):
                at = at_piece(i)
                size = jnp.abs(delta[l, k, :, at].astype(F32))
                sums[k, l : l + 1, at] = jnp.sum(size, axis=0, keepdims=True)
                return carry

            lax.fori_loop(0, pieces, add_up, 0)

    def hold_own(l):
        def body(i, carry):
            at = at_piece(i)
            own_kept[l, :, at] = masked(l, 0, at)
            return carry

        lax.fori_loop(0, pieces, body, 0)

    hold_own(0)
    for bit in range(group_bits):
        copy = pltpu.make_async_remote_copy(
            src_ref=sums, dst_ref=sums_in.at[bit],
            send_sem=sums_sem.at[bit, 0], recv_sem=sums_sem.at[bit, 1],
            device_id={"shard": xor_peer(bit)}, device_id_type=MESH,
        )
        copy.start()
        copy.wait()
        for k in range(tasks):

            def join(i, carry, k=k, bit=bit):
                at = at_piece(i)
                sums[k, :, at] = sums[k, :, at] + sums_in[bit, k, :, at]
                return carry

            lax.fori_loop(0, pieces, join, 0)

    total = jnp.zeros((layers, 128), F32)
    for k in range(tasks):

        def gather(i, carry, k=k):
            block = sums[k, :, at_piece(i)]
            for j in range(piece // 128):
                carry = carry + block[:, j * 128 : (j + 1) * 128]
            return carry

        total = lax.fori_loop(0, pieces, gather, total)

    for step, bit in enumerate(range(group_bits, all_bits)):
        part[step] = total
        if step + 1 < layers:
            hold_own(step + 1)
        copy = pltpu.make_async_remote_copy(
            src_ref=part.at[step], dst_ref=part_in.at[step],
            send_sem=part_sem.at[step, 0], recv_sem=part_sem.at[step, 1],
            device_id={"shard": xor_peer(bit)}, device_id_type=MESH,
        )
        copy.start()
        copy.wait()
        total = total + part_in[step]
    for l in range(all_bits - group_bits + 1, layers):
        hold_own(l)
    grand_mean = jnp.sum(total, axis=1, keepdims=True) / (EXPERTS * row_total * width)

    for k in list(range(1, tasks)) + [0]:

        def rate(i, carry, k=k):
            at = at_piece(i)
            mean = sums[k, :, at] / row_total
            keep = (0.2 + 0.7 * mean / (mean + grand_mean)).astype(jnp.bfloat16)
            if k:
                chance[k - 1, :, at] = keep
            else:
                own_rate[:, at] = 1.0 / keep.astype(F32)
            return carry

        lax.fori_loop(0, pieces, rate, 0)
    chances = []
    segment = columns // groups
    mine = pl.ds(pl.multiple_of(lax.rem(me_shard, groups) * segment, 128), segment)
    for k in range(1, tasks):
        copy = pltpu.make_async_remote_copy(
            src_ref=chance.at[k - 1, :, mine], dst_ref=chance_in.at[k - 1, :, mine],
            send_sem=chance_sem.at[k - 1, 0], recv_sem=chance_sem.at[k - 1, 1],
            device_id={"task": task_peer(k)}, device_id_type=MESH,
        )
        copy.start()
        chances.append(copy)
    while ready:
        start_send(*ready.pop(0))

    for l in range(layers):

        def rescale(i, carry, l=l):
            at = at_piece(i)
            own_kept[l, :, at] = own_kept[l, :, at] * own_rate[l : l + 1, at]
            return carry

        lax.fori_loop(0, pieces, rescale, 0)

    shares = {}
    for k in range(1, tasks):
        chances[k - 1].wait()
        for mask in range(1, groups):
            copy = pltpu.make_async_remote_copy(
                src_ref=chance_in.at[k - 1, :, mine], dst_ref=chance_in.at[k - 1, :, mine],
                send_sem=share_sem.at[k - 1, mask - 1, 0], recv_sem=share_sem.at[k - 1, mask - 1, 1],
                device_id={"shard": flipped(me_shard, mask)}, device_id_type=MESH,
            )
            copy.start()
            shares[k, mask] = copy
    for k in range(1, tasks):
        for mask in range(1, groups):
            shares[k, mask].wait()

        def invert(i, carry, k=k):
            at = at_piece(i)
            in_rate[k - 1, :, at] = 1.0 / chance_in[k - 1, :, at].astype(F32)
            return carry

        lax.fori_loop(0, pieces, invert, 0)

    for l in range(layers):
        for i in range(pieces):
            at = at_piece(i)
            value = own_kept[l, :, at]
            for k in range(1, tasks):
                sends[l, k, i].wait()
                value = value + incoming[l, k - 1, :, at].astype(F32) * in_rate[k - 1, l : l + 1, at]
            merged[l, :, at] = value.astype(jnp.bfloat16)


def put_out(value, out_hbm, sem):
    copy = pltpu.make_async_copy(value, out_hbm, sem)
    copy.start()
    copy.wait()


def on_device(task_deltas, rank_scores, keep_limits):
    tasks, shards = lax.axis_size("task"), lax.axis_size("shard")
    _, layers, rows, width = task_deltas.shape
    columns = width // tasks
    pieces = columns // min(4096, columns)
    others = max(tasks - 1, 1)
    groups = shards // EXPERTS
    group_bits = max(groups.bit_length() - 1, 1)
    rest_bits = max(shards.bit_length() - groups.bit_length(), 1)
    half = jnp.bfloat16
    dma = pltpu.SemaphoreType.DMA
    keep_limits = pltpu.with_memory_space_constraint(keep_limits, pltpu.HBM)
    result = pl.pallas_call(
        functools.partial(kernel, (layers, rows, width, tasks, shards)),
        out_shape=jax.ShapeDtypeStruct((layers, rows, columns), half),
        in_specs=[
            pl.BlockSpec(memory_space=pltpu.HBM),
            pl.BlockSpec(memory_space=pltpu.HBM),
            pl.BlockSpec(memory_space=pltpu.HBM),
        ],
        out_specs=pl.BlockSpec(memory_space=pltpu.VMEM),
        scratch_shapes=[
            pltpu.SMEM(keep_limits.shape[1:], jnp.int32),
            pltpu.VMEM((layers, tasks, rows, columns), half),
            pltpu.VMEM((layers, tasks, rows, columns), jnp.int32),
            pltpu.VMEM((layers, others, rows, columns), half),
            pltpu.VMEM((layers, others, rows, columns), half),
            pltpu.VMEM((tasks, layers, columns), F32),
            pltpu.VMEM((group_bits, tasks, layers, columns), F32),
            pltpu.VMEM((rest_bits, layers, 128), F32),
            pltpu.VMEM((rest_bits, layers, 128), F32),
            pltpu.VMEM((others, layers, columns), half),
            pltpu.VMEM((others, layers, columns), half),
            pltpu.VMEM((layers, columns), F32),
            pltpu.VMEM((others, layers, columns), F32),
            pltpu.VMEM((layers, rows, columns), F32),
            dma(()),
            dma((layers, tasks, pieces, 2)),
            dma((layers, others, pieces)),
            dma((layers, others, pieces)),
            dma((group_bits, 2)),
            dma((rest_bits, 2)),
            dma((others, 2)),
            dma((others, max(groups - 1, 1), 2)),
        ],
        compiler_params=pltpu.CompilerParams(
            collective_id=0, has_side_effects=True, vmem_limit_bytes=52 * 2**20
        ),
        name="merge",
    )(task_deltas, rank_scores, keep_limits)
    return pl.pallas_call(
        put_out,
        out_shape=jax.ShapeDtypeStruct(result.shape, result.dtype),
        in_specs=[pl.BlockSpec(memory_space=pltpu.VMEM)],
        out_specs=pl.BlockSpec(memory_space=pltpu.HBM),
        scratch_shapes=[dma(())],
        compiler_params=pltpu.CompilerParams(vmem_limit_bytes=4 * 2**20),
        name="put",
    )(result)


def solution(mesh):
    return jax.shard_map(
        on_device,
        mesh=mesh,
        in_specs=(
            P("task", None, "shard", None),
            P("task", None, "shard", None),
            P("task", None, None),
        ),
        out_specs=P(None, "shard", "task"),
        check_vma=False,
    )
```

profile of v0, /device:TPU:0, one launch (start us, length us, event | category | flops | bytes accessed | tf_op | source)
XLA Modules:
  0.0 30.7 jit_solution(13288653833919866466)
XLA Ops:
  0.0 29.7 %merge.1.value = bf16[4,16,8192]{2,1,0:T(8,128)(2,1)S(1)} custom-call(bf16[1,4,16,16384]{3,2,1,0:T(8,128)(2,1)} %delta_hbm.1, s32[1,4,16,16384]{3,2,1,0:T(8,128)} %score_hbm.1, s32[1,4,8]{2,1,0:T(4,128)} %limit_hbm.1), custom_call_target="tpu_custom_call" | custom-call | tf_op jit(solution)/shard_map/merge/pallas_call | solution.py:273
  29.7 1.0 %put.1 = bf16[4,16,8192]{2,1,0:T(8,128)(2,1)} custom-call(bf16[4,16,8192]{2,1,0:T(8,128)(2,1)S(1)} %merge.1.value), custom_call_target="tpu_custom_call" | custom-call | tf_op jit(solution)/shard_map/put/pallas_call | solution.py:311
where the time goes:
time: 30.9 us; the launch traced here: 30.7 us
  Pallas kernels  30.7 us (99%)
    pallas_call x1, Pallas kernels, on_device(): pl.pallas_call(functools.partial(kernel, (layers, rows, width, tasks, sha...  29.7 us
    pallas_call x1, Pallas kernels, on_device(): pl.pallas_call(put_out, out_shape=jax.ShapeDtypeStruct(result.shape, resu...  0.98 us

commit v1 on v0

v1 whole, which is shorter than its diff:
```python
import functools
import jax
import jax.numpy as jnp
from jax import lax
from jax.experimental import pallas as pl
from jax.experimental.pallas import tpu as pltpu
from jax.sharding import PartitionSpec as P

EXPERTS = 8
F32 = jnp.float32
BF16 = jnp.bfloat16
MESH = pl.DeviceIdType.MESH
BF16_MAX = float(jnp.finfo(BF16).max)
F32_MAX = float(jnp.finfo(F32).max)


def plan(layers, columns, tasks, groups):
    unit = 128 * groups
    raw = columns // 2 // unit * unit
    first = min(1024, raw // 2 // 128 * 128)
    last = min(1024, (columns - raw) // 2 // 128 * 128)
    raw_units, scaled_units = [], []
    for l in range(layers):
        for k in range(1, tasks):
            if l == 0 and k == 1:
                raw_units += [(l, k, 0, first), (l, k, first, raw - first)]
            else:
                raw_units.append((l, k, 0, raw))
            if l == layers - 1:
                cut = columns - last
                scaled_units += [(l, k, raw, cut - raw), (l, k, cut, last)]
            else:
                scaled_units.append((l, k, raw, columns - raw))
    return raw, raw_units, scaled_units


def low_size(shards):
    return 2 ** ((shards.bit_length()) // 2)


def contact_masks(shards):
    low = low_size(shards)
    return list(range(1, low)) + [low * j for j in range(1, shards // low)]


def kernel(
    sizes, delta_hbm, score_hbm, limit_hbm, merged,
    limit_ref, delta, score, outgoing, incoming, sums, sums_in, part, part_in, wide, wide_in,
    chance, chance_in, own_rate, out_rate, in_rate, own,
    limit_sem, unit_sem, rest_sem, send_sem, recv_sem, seen_sem,
    sums_sem, part_sem, wide_sem, chance_sem, share_sem,
):
    layers, rows, width, tasks, shards = sizes
    columns = width // tasks
    groups = shards // EXPERTS
    low = low_size(shards)
    all_bits = shards.bit_length() - 1
    raw, raw_units, scaled_units = plan(layers, columns, tasks, groups)
    contacts = contact_masks(shards)
    me_shard, me_task = lax.axis_index("shard"), lax.axis_index("task")
    expert = me_shard // groups
    row_total = rows * groups
    late_core = lax.rem(me_shard, 2) == 1

    def flipped(mask):
        index = me_shard
        for bit in range(all_bits):
            stride = 2**bit
            if mask & stride:
                index = index + stride * (1 - 2 * lax.rem(me_shard // stride, 2))
        return index

    def task_peer(k):
        return lax.rem(me_task + k, tasks)

    def upper(mask):
        return lax.rem(me_shard // 2 ** (mask.bit_length() - 1), 2)

    def greet(sem, mask):
        pl.semaphore_signal(sem, inc=1, device_id={"shard": flipped(mask)}, device_id_type=MESH)

    def sweep(start, length, body):
        step = length
        while step > 2048:
            step //= 2
        if step % 128:
            step = 128

        def turn(i, carry):
            body(pl.ds(pl.multiple_of(start + i * step, 128), step))
            return carry

        if length == step:
            body(pl.ds(start, length))
        else:
            lax.fori_loop(0, length // step, turn, 0)

    barrier = pltpu.get_barrier_semaphore()
    for k in range(1, tasks):
        pl.semaphore_signal(barrier, inc=1, device_id={"task": task_peer(k)}, device_id_type=MESH)

    limit_copy = pltpu.make_async_copy(limit_hbm.at[0], limit_ref, limit_sem)
    limit_copy.start()
    unit_loads = []
    for u, (l, k, c, n) in enumerate(raw_units):
        there = pl.ds(pl.multiple_of(task_peer(k) * columns + c, 128), n)
        unit_loads.append([
            pltpu.make_async_copy(whole.at[0, l, :, there], held.at[k, l, :, pl.ds(c, n)], unit_sem.at[u, j])
            for j, (whole, held) in enumerate(((score_hbm, score), (delta_hbm, delta)))
        ])
        for copy in unit_loads[u]:
            copy.start()
    rest_loads = {}
    for j, (whole, held) in enumerate(((delta_hbm, delta), (score_hbm, score))):
        for k in list(range(1, tasks)) + [0]:
            c = raw if k else 0
            there = pl.ds(pl.multiple_of(task_peer(k) * columns + c, 128), columns - c)
            rest_loads[j, k] = pltpu.make_async_copy(
                whole.at[0, :, :, there], held.at[k, :, :, pl.ds(c, columns - c)], rest_sem.at[j, k]
            )
            rest_loads[j, k].start()

    for mask in contacts:
        @pl.when(upper(mask) == 0)
        def _(mask=mask):
            greet(barrier, mask)

    def masked(l, k, at):
        limit = limit_ref[l, expert]
        return jnp.where(score[k, l, :, at] < limit, delta[k, l, :, at].astype(F32), 0.0)

    sends = []
    for u, (l, k, c, n) in enumerate(raw_units + scaled_units):
        sends.append(pltpu.make_async_remote_copy(
            src_ref=outgoing.at[k - 1, l, :, pl.ds(c, n)],
            dst_ref=incoming.at[k - 1, l, :, pl.ds(c, n)],
            send_sem=send_sem.at[u], recv_sem=recv_sem.at[u],
            device_id={"task": task_peer(k)}, device_id_type=MESH,
        ))

    limit_copy.wait()
    early = 2
    for u, (l, k, c, n) in enumerate(raw_units):
        for copy in unit_loads[u]:
            copy.wait()

        def prepare(at, l=l, k=k):
            outgoing[k - 1, l, :, at] = masked(l, k, at).astype(BF16)

        sweep(c, n, prepare)
        if u == 0:
            pl.semaphore_wait(barrier, tasks - 1 + sum(upper(mask) for mask in contacts))
        if u < early:
            sends[u].start()
        else:
            @pl.when(jnp.logical_not(late_core))
            def _(u=u):
                sends[u].start()
        if u == 0:
            for j, mask in enumerate(contacts):
                @pl.when(upper(mask) == 1)
                def _(j=j, mask=mask):
                    greet(seen_sem.at[j], mask)

    total = jnp.zeros((layers, 128), F32)
    for k in range(tasks):
        rest_loads[0, k].wait()
        for l in range(layers):

            def add_up(at, l=l, k=k):
                size = jnp.abs(delta[k, l, :, at].astype(F32))
                sums[k, l : l + 1, at] = jnp.sum(size, axis=0, keepdims=True)

            sweep(0, columns, add_up)
    step = min(2048, columns)
    for k in range(tasks):

        def gather(i, carry, k=k):
            block = sums[k, :, pl.ds(pl.multiple_of(i * step, 128), step)]
            for j in range(step // 128):
                carry = carry + block[:, j * 128 : (j + 1) * 128]
            return carry

        total = lax.fori_loop(0, columns // step, gather, total)
    part[...] = total

    for j, mask in enumerate(contacts):
        @pl.when(upper(mask) == 0)
        def _(j=j):
            pl.semaphore_wait(seen_sem.at[j], 1)

    def exchange(src, dst, sems, mask):
        copy = pltpu.make_async_remote_copy(
            src_ref=src, dst_ref=dst, send_sem=sems.at[0], recv_sem=sems.at[1],
            device_id={"shard": flipped(mask)}, device_id_type=MESH,
        )
        copy.start()
        return copy

    near = [exchange(part, part_in.at[m - 1], part_sem.at[m - 1], m) for m in range(1, low)]
    pairs = [exchange(sums, sums_in.at[m - 1], sums_sem.at[m - 1], m) for m in range(1, groups)]

    for u in range(early, len(raw_units)):
        @pl.when(late_core)
        def _(u=u):
            sends[u].start()

    for m, copy in enumerate(near):
        copy.wait()
        total = total + part_in[m]
    wide[...] = total
    far = [
        exchange(wide, wide_in.at[j - 1], wide_sem.at[j - 1], low * j) for j in range(1, shards // low)
    ]
    for copy in pairs:
        copy.wait()
    for k in range(tasks):

        def join(at, k=k):
            value = sums[k, :, at]
            for m in range(groups - 1):
                value = value + sums_in[m, k, :, at]
            sums[k, :, at] = value

        sweep(0, columns, join)
    for j, copy in enumerate(far):
        copy.wait()
        total = total + wide_in[j]
    grand_mean = jnp.sum(total, axis=1, keepdims=True) / (EXPERTS * row_total * width)

    def keep(k, at):
        mean = sums[k, :, at] / row_total
        return (0.2 + 0.7 * mean / (mean + grand_mean)).astype(BF16)

    segment = raw // groups
    mine = pl.ds(pl.multiple_of(lax.rem(me_shard, groups) * segment, 128), segment)
    chances = []
    for k in range(1, tasks):

        def fill(at, k=k):
            chance[k - 1, :, at] = keep(k, at)

        sweep(0, raw, fill)

        def invert_out(at, k=k):
            out_rate[k - 1, :, at] = 1.0 / keep(k, at).astype(F32)

        sweep(raw, columns - raw, invert_out)
        copy = pltpu.make_async_remote_copy(
            src_ref=chance.at[k - 1, :, mine], dst_ref=chance_in.at[k - 1, :, mine],
            send_sem=chance_sem.at[k - 1, 0], recv_sem=chance_sem.at[k - 1, 1],
            device_id={"task": task_peer(k)}, device_id_type=MESH,
        )
        copy.start()
        chances.append(copy)

    for k in range(1, tasks):
        rest_loads[1, k].wait()
    for u, (l, k, c, n) in enumerate(scaled_units):

        def rescale(at, l=l, k=k):
            value = masked(l, k, at) * out_rate[k - 1, l : l + 1, at]
            held = jnp.clip(value, -BF16_MAX, BF16_MAX)
            outgoing[k - 1, l, :, at] = jnp.where(jnp.abs(value) <= F32_MAX, held, value).astype(BF16)

        sweep(c, n, rescale)
        sends[len(raw_units) + u].start()

    rest_loads[1, 0].wait()

    def invert_own(at):
        own_rate[:, at] = 1.0 / keep(0, at).astype(F32)

    sweep(0, columns, invert_own)
    for l in range(layers):

        def hold(at, l=l):
            own[l, :, at] = masked(l, 0, at) * own_rate[l : l + 1, at]

        sweep(0, columns, hold)

    shares = []
    for k in range(1, tasks):
        chances[k - 1].wait()
        for mask in range(1, groups):
            shares.append(exchange(
                chance_in.at[k - 1, :, mine], chance_in.at[k - 1, :, mine], share_sem.at[k - 1, mask - 1], mask
            ))
    for copy in shares:
        copy.wait()
    for k in range(1, tasks):

        def invert_in(at, k=k):
            in_rate[k - 1, :, at] = 1.0 / chance_in[k - 1, :, at].astype(F32)

        sweep(0, raw, invert_in)

    for u, (l, k, c, n) in enumerate(raw_units):
        sends[u].wait()

        def add_raw(at, l=l, k=k):
            own[l, :, at] = own[l, :, at] + incoming[k - 1, l, :, at].astype(F32) * in_rate[k - 1, l : l + 1, at]

        if k < tasks - 1:
            sweep(c, n, add_raw)
            continue

        def end_raw(at, l=l, k=k):
            value = own[l, :, at] + incoming[k - 1, l, :, at].astype(F32) * in_rate[k - 1, l : l + 1, at]
            merged[l, :, at] = value.astype(BF16)

        sweep(c, n, end_raw)

    for u, (l, k, c, n) in enumerate(scaled_units):
        sends[len(raw_units) + u].wait()

        def add_scaled(at, l=l, k=k):
            own[l, :, at] = own[l, :, at] + incoming[k - 1, l, :, at].astype(F32)

        def end_scaled(at, l=l, k=k):
            merged[l, :, at] = (own[l, :, at] + incoming[k - 1, l, :, at].astype(F32)).astype(BF16)

        sweep(c, n, add_scaled if k < tasks - 1 else end_scaled)


def put_out(value, out_hbm, sem):
    copy = pltpu.make_async_copy(value, out_hbm, sem)
    copy.start()
    copy.wait()


def on_device(task_deltas, rank_scores, keep_limits):
    tasks, shards = lax.axis_size("task"), lax.axis_size("shard")
    _, layers, rows, width = task_deltas.shape
    columns = width // tasks
    others = max(tasks - 1, 1)
    groups = shards // EXPERTS
    low = low_size(shards)
    raw, raw_units, scaled_units = plan(layers, columns, tasks, groups)
    sent = len(raw_units) + len(scaled_units)
    dma = pltpu.SemaphoreType.DMA
    keep_limits = pltpu.with_memory_space_constraint(keep_limits, pltpu.HBM)
    result = pl.pallas_call(
        functools.partial(kernel, (layers, rows, width, tasks, shards)),
        out_shape=jax.ShapeDtypeStruct((layers, rows, columns), BF16),
        in_specs=[
            pl.BlockSpec(memory_space=pltpu.HBM),
            pl.BlockSpec(memory_space=pltpu.HBM),
            pl.BlockSpec(memory_space=pltpu.HBM),
        ],
        out_specs=pl.BlockSpec(memory_space=pltpu.VMEM),
        scratch_shapes=[
            pltpu.SMEM(keep_limits.shape[1:], jnp.int32),
            pltpu.VMEM((tasks, layers, rows, columns), BF16),
            pltpu.VMEM((tasks, layers, rows, columns), jnp.int32),
            pltpu.VMEM((others, layers, rows, columns), BF16),
            pltpu.VMEM((others, layers, rows, columns), BF16),
            pltpu.VMEM((tasks, layers, columns), F32),
            pltpu.VMEM((max(groups - 1, 1), tasks, layers, columns), F32),
            pltpu.VMEM((layers, 128), F32),
            pltpu.VMEM((max(low - 1, 1), layers, 128), F32),
            pltpu.VMEM((layers, 128), F32),
            pltpu.VMEM((max(shards // low - 1, 1), layers, 128), F32),
            pltpu.VMEM((others, layers, raw), BF16),
            pltpu.VMEM((others, layers, raw), BF16),
            pltpu.VMEM((layers, columns), F32),
            pltpu.VMEM((others, layers, columns), F32),
            pltpu.VMEM((others, layers, raw), F32),
            pltpu.VMEM((layers, rows, columns), F32),
            dma(()),
            dma((len(raw_units), 2)),
            dma((2, tasks)),
            dma((sent,)),
            dma((sent,)),
            pltpu.SemaphoreType.REGULAR((len(contact_masks(shards)),)),
            dma((max(groups - 1, 1), 2)),
            dma((max(low - 1, 1), 2)),
            dma((max(shards // low - 1, 1), 2)),
            dma((others, 2)),
            dma((others, max(groups - 1, 1), 2)),
        ],
        compiler_params=pltpu.CompilerParams(
            collective_id=0, has_side_effects=True, vmem_limit_bytes=52 * 2**20
        ),
        name="merge",
    )(task_deltas, rank_scores, keep_limits)
    return pl.pallas_call(
        put_out,
        out_shape=jax.ShapeDtypeStruct(result.shape, result.dtype),
        in_specs=[pl.BlockSpec(memory_space=pltpu.VMEM)],
        out_specs=pl.BlockSpec(memory_space=pltpu.HBM),
        scratch_shapes=[dma(())],
        compiler_params=pltpu.CompilerParams(vmem_limit_bytes=4 * 2**20),
        name="put",
    )(result)


def solution(mesh):
    return jax.shard_map(
        on_device,
        mesh=mesh,
        in_specs=(
            P("task", None, "shard", None),
            P("task", None, "shard", None),
            P("task", None, None),
        ),
        out_specs=P(None, "shard", "task"),
        check_vma=False,
    )
```

time: 30.9 us -> 29 us (0.939)
  Pallas kernels: 30.7 us -> 28.9 us
    pallas_call x1, Pallas kernels: 29.7 us -> 27.9 us  [on_device(): pl.pallas_call(functools.partial(kernel, (layers, rows, width, tasks, sha...]
where the time goes in v1:
time: 29 us; the launch traced here: 28.9 us
  Pallas kernels  28.9 us (100%)
    pallas_call x1, Pallas kernels, on_device(): pl.pallas_call(functools.partial(kernel, (layers, rows, width, tasks, sha...  27.9 us
    pallas_call x1, Pallas kernels, on_device(): pl.pallas_call(put_out, out_shape=jax.ShapeDtypeStruct(result.shape, resu...  0.98 us

profile of v1, /device:TPU:0, one launch (start us, length us, event | category | flops | bytes accessed | tf_op | source)
XLA Modules:
  0.0 28.9 jit_solution(10236110889864860884)
XLA Ops:
  0.0 27.9 %merge.1.value = bf16[4,16,8192]{2,1,0:T(8,128)(2,1)S(1)} custom-call(bf16[1,4,16,16384]{3,2,1,0:T(8,128)(2,1)} %delta_hbm.1, s32[1,4,16,16384]{3,2,1,0:T(8,128)} %score_hbm.1, s32[1,4,8]{2,1,0:T(4,128)} %limit_hbm.1), custom_call_target="tpu_custom_call" | custom-call | tf_op jit(solution)/shard_map/merge/pallas_call | solution.py:343
  27.9 1.0 %put.1 = bf16[4,16,8192]{2,1,0:T(8,128)(2,1)} custom-call(bf16[4,16,8192]{2,1,0:T(8,128)(2,1)S(1)} %merge.1.value), custom_call_target="tpu_custom_call" | custom-call | tf_op jit(solution)/shard_map/put/pallas_call | solution.py:387

commit v2 on v1

--- a/solution.py
+++ b/solution.py
@@ -14,16 +14,19 @@
 F32_MAX = float(jnp.finfo(F32).max)
 
 
+HUB = 1
+
+
 def plan(layers, columns, tasks, groups):
     unit = 128 * groups
     raw = columns // 2 // unit * unit
-    first = min(1024, raw // 2 // 128 * 128)
+    first = min(1024, raw // 4 // 128 * 128)
     last = min(1024, (columns - raw) // 2 // 128 * 128)
     raw_units, scaled_units = [], []
     for l in range(layers):
         for k in range(1, tasks):
             if l == 0 and k == 1:
-                raw_units += [(l, k, 0, first), (l, k, first, raw - first)]
+                raw_units += [(l, k, 0, first), (l, k, first, first), (l, k, 2 * first, raw - 2 * first)]
             else:
                 raw_units.append((l, k, 0, raw))
             if l == layers - 1:
@@ -34,33 +37,24 @@
     return raw, raw_units, scaled_units
 
 
-def low_size(shards):
-    return 2 ** ((shards.bit_length()) // 2)
-
-
-def contact_masks(shards):
-    low = low_size(shards)
-    return list(range(1, low)) + [low * j for j in range(1, shards // low)]
-
-
 def kernel(
     sizes, delta_hbm, score_hbm, limit_hbm, merged,
-    limit_ref, delta, score, outgoing, incoming, sums, sums_in, part, part_in, wide, wide_in,
+    limit_ref, delta, score, outgoing, incoming, sums, sums_in, part, part_in, total_ref,
     chance, chance_in, own_rate, out_rate, in_rate, own,
-    limit_sem, unit_sem, rest_sem, send_sem, recv_sem, seen_sem,
-    sums_sem, part_sem, wide_sem, chance_sem, share_sem,
+    limit_sem, unit_sem, later_sem, rest_sem, send_sem, recv_sem,
+    sums_sem, part_send, part_recv, total_send, total_recv, chance_sem, share_sem,
 ):
     layers, rows, width, tasks, shards = sizes
     columns = width // tasks
     groups = shards // EXPERTS
-    low = low_size(shards)
     all_bits = shards.bit_length() - 1
     raw, raw_units, scaled_units = plan(layers, columns, tasks, groups)
-    contacts = contact_masks(shards)
     me_shard, me_task = lax.axis_index("shard"), lax.axis_index("task")
     expert = me_shard // groups
     row_total = rows * groups
     late_core = lax.rem(me_shard, 2) == 1
+    is_hub = me_shard == HUB
+    outside = [s for s in range(shards) if s // groups != HUB // groups]
 
     def flipped(mask):
         index = me_shard
@@ -73,12 +67,6 @@
     def task_peer(k):
         return lax.rem(me_task + k, tasks)
 
-    def upper(mask):
-        return lax.rem(me_shard // 2 ** (mask.bit_length() - 1), 2)
-
-    def greet(sem, mask):
-        pl.semaphore_signal(sem, inc=1, device_id={"shard": flipped(mask)}, device_id_type=MESH)
-
     def sweep(start, length, body):
         step = length
         while step > 2048:
@@ -98,32 +86,44 @@
     barrier = pltpu.get_barrier_semaphore()
     for k in range(1, tasks):
         pl.semaphore_signal(barrier, inc=1, device_id={"task": task_peer(k)}, device_id_type=MESH)
+    for mask in range(1, groups):
+        pl.semaphore_signal(barrier, inc=1, device_id={"shard": flipped(mask)}, device_id_type=MESH)
 
     limit_copy = pltpu.make_async_copy(limit_hbm.at[0], limit_ref, limit_sem)
     limit_copy.start()
-    unit_loads = []
+
+    def load(whole, held, k, ls, c, n, sem):
+        there = pl.ds(pl.multiple_of(task_peer(k) * columns + c, 128), n)
+        copy = pltpu.make_async_copy(whole.at[0, ls, :, there], held.at[k, ls, :, pl.ds(c, n)], sem)
+        copy.start()
+        return copy
+
+    every, later = pl.ds(0, layers), pl.ds(1, layers - 1)
+    unit_loads = {}
     for u, (l, k, c, n) in enumerate(raw_units):
-        there = pl.ds(pl.multiple_of(task_peer(k) * columns + c, 128), n)
-        unit_loads.append([
-            pltpu.make_async_copy(whole.at[0, l, :, there], held.at[k, l, :, pl.ds(c, n)], unit_sem.at[u, j])
-            for j, (whole, held) in enumerate(((score_hbm, score), (delta_hbm, delta)))
-        ])
-        for copy in unit_loads[u]:
-            copy.start()
-    rest_loads = {}
-    for j, (whole, held) in enumerate(((delta_hbm, delta), (score_hbm, score))):
-        for k in list(range(1, tasks)) + [0]:
-            c = raw if k else 0
-            there = pl.ds(pl.multiple_of(task_peer(k) * columns + c, 128), columns - c)
-            rest_loads[j, k] = pltpu.make_async_copy(
-                whole.at[0, :, :, there], held.at[k, :, :, pl.ds(c, columns - c)], rest_sem.at[j, k]
-            )
-            rest_loads[j, k].start()
-
-    for mask in contacts:
-        @pl.when(upper(mask) == 0)
-        def _(mask=mask):
-            greet(barrier, mask)
+        if l == 0:
+            unit_loads[u] = [
+                load(score_hbm, score, k, l, c, n, unit_sem.at[u, 0]),
+                load(delta_hbm, delta, k, l, c, n, unit_sem.at[u, 1]),
+            ]
+    later_loads = {k: load(delta_hbm, delta, k, later, 0, columns, later_sem.at[k]) for k in range(1, tasks)}
+    for u, (l, k, c, n) in enumerate(raw_units):
+        if l:
+            unit_loads[u] = [load(score_hbm, score, k, l, c, n, unit_sem.at[u, 0])]
+    delta_loads = [
+        load(delta_hbm, delta, k, 0, raw, columns - raw, rest_sem.at[0, k]) if k
+        else load(delta_hbm, delta, 0, every, 0, columns, rest_sem.at[0, 0])
+        for k in list(range(1, tasks)) + [0]
+    ]
+    score_loads = {
+        k: load(score_hbm, score, k, every, raw if k else 0, columns - (raw if k else 0), rest_sem.at[1, k])
+        for k in list(range(1, tasks)) + [0]
+    }
+
+    @pl.when(is_hub)
+    def _():
+        for s in outside:
+            pl.semaphore_signal(barrier, inc=1, device_id={"shard": s}, device_id_type=MESH)
 
     def masked(l, k, at):
         limit = limit_ref[l, expert]
@@ -141,6 +141,10 @@
     limit_copy.wait()
     early = 2
     for u, (l, k, c, n) in enumerate(raw_units):
+        if l and later_loads:
+            for copy in later_loads.values():
+                copy.wait()
+            later_loads = None
         for copy in unit_loads[u]:
             copy.wait()
 
@@ -149,22 +153,19 @@
 
         sweep(c, n, prepare)
         if u == 0:
-            pl.semaphore_wait(barrier, tasks - 1 + sum(upper(mask) for mask in contacts))
+            away = jnp.where(expert == HUB // groups, 0, 1)
+            pl.semaphore_wait(barrier, tasks - 1 + groups - 1 + away)
         if u < early:
             sends[u].start()
         else:
             @pl.when(jnp.logical_not(late_core))
             def _(u=u):
                 sends[u].start()
-        if u == 0:
-            for j, mask in enumerate(contacts):
-                @pl.when(upper(mask) == 1)
-                def _(j=j, mask=mask):
-                    greet(seen_sem.at[j], mask)
 
     total = jnp.zeros((layers, 128), F32)
+    for copy in delta_loads:
+        copy.wait()
     for k in range(tasks):
-        rest_loads[0, k].wait()
         for l in range(layers):
 
             def add_up(at, l=l, k=k):
@@ -183,11 +184,6 @@
 
         total = lax.fori_loop(0, columns // step, gather, total)
     part[...] = total
-
-    for j, mask in enumerate(contacts):
-        @pl.when(upper(mask) == 0)
-        def _(j=j):
-            pl.semaphore_wait(seen_sem.at[j], 1)
 
     def exchange(src, dst, sems, mask):
         copy = pltpu.make_async_remote_copy(
@@ -197,21 +193,26 @@
         copy.start()
         return copy
 
-    near = [exchange(part, part_in.at[m - 1], part_sem.at[m - 1], m) for m in range(1, low)]
     pairs = [exchange(sums, sums_in.at[m - 1], sums_sem.at[m - 1], m) for m in range(1, groups)]
+
+    def to_shard(src, dst, send, recv, s):
+        return pltpu.make_async_remote_copy(
+            src_ref=src, dst_ref=dst, send_sem=send, recv_sem=recv, device_id={"shard": s}, device_id_type=MESH
+        )
+
+    others = [s for s in range(shards) if s != HUB]
+    to_hub = to_shard(part, part_in.at[me_shard], part_send, part_recv.at[me_shard], HUB)
+    to_all = {s: to_shard(total_ref, total_ref, total_send.at[s], total_recv, s) for s in others}
+
+    @pl.when(jnp.logical_not(is_hub))
+    def _():
+        to_hub.start()
 
     for u in range(early, len(raw_units)):
         @pl.when(late_core)
         def _(u=u):
             sends[u].start()
 
-    for m, copy in enumerate(near):
-        copy.wait()
-        total = total + part_in[m]
-    wide[...] = total
-    far = [
-        exchange(wide, wide_in.at[j - 1], wide_sem.at[j - 1], low * j) for j in range(1, shards // low)
-    ]
     for copy in pairs:
         copy.wait()
     for k in range(tasks):
@@ -223,9 +224,22 @@
             sums[k, :, at] = value
 
         sweep(0, columns, join)
-    for j, copy in enumerate(far):
-        copy.wait()
-        total = total + wide_in[j]
+    @pl.when(is_hub)
+    def _():
+        value = part[...]
+        for s in others:
+            to_shard(part, part_in.at[s], part_send, part_recv.at[s], s).wait_recv()
+            value = value + part_in[s]
+        total_ref[...] = value
+        for s in others:
+            to_all[s].start()
+
+    @pl.when(jnp.logical_not(is_hub))
+    def _():
+        to_all[others[0]].wait_recv()
+        to_hub.wait_send()
+
+    total = total_ref[...]
     grand_mean = jnp.sum(total, axis=1, keepdims=True) / (EXPERTS * row_total * width)
 
     def keep(k, at):
@@ -255,7 +269,7 @@
         chances.append(copy)
 
     for k in range(1, tasks):
-        rest_loads[1, k].wait()
+        score_loads[k].wait()
     for u, (l, k, c, n) in enumerate(scaled_units):
 
         def rescale(at, l=l, k=k):
@@ -266,7 +280,7 @@
         sweep(c, n, rescale)
         sends[len(raw_units) + u].start()
 
-    rest_loads[1, 0].wait()
+    score_loads[0].wait()
 
     def invert_own(at):
         own_rate[:, at] = 1.0 / keep(0, at).astype(F32)
@@ -311,6 +325,11 @@
 
         sweep(c, n, end_raw)
 
+    @pl.when(is_hub)
+    def _():
+        for s in others:
+            to_all[s].wait_send()
+
     for u, (l, k, c, n) in enumerate(scaled_units):
         sends[len(raw_units) + u].wait()
 
@@ -335,7 +354,6 @@
     columns = width // tasks
     others = max(tasks - 1, 1)
     groups = shards // EXPERTS
-    low = low_size(shards)
     raw, raw_units, scaled_units = plan(layers, columns, tasks, groups)
     sent = len(raw_units) + len(scaled_units)
     dma = pltpu.SemaphoreType.DMA
@@ -358,9 +376,8 @@
             pltpu.VMEM((tasks, layers, columns), F32),
             pltpu.VMEM((max(groups - 1, 1), tasks, layers, columns), F32),
             pltpu.VMEM((layers, 128), F32),
-            pltpu.VMEM((max(low - 1, 1), layers, 128), F32),
+            pltpu.VMEM((shards, layers, 128), F32),
             pltpu.VMEM((layers, 128), F32),
-            pltpu.VMEM((max(shards // low - 1, 1), layers, 128), F32),
             pltpu.VMEM((others, layers, raw), BF16),
             pltpu.VMEM((others, layers, raw), BF16),
             pltpu.VMEM((layers, columns), F32),
@@ -369,13 +386,15 @@
             pltpu.VMEM((layers, rows, columns), F32),
             dma(()),
             dma((len(raw_units), 2)),
+            dma((tasks,)),
             dma((2, tasks)),
             dma((sent,)),
             dma((sent,)),
-            pltpu.SemaphoreType.REGULAR((len(contact_masks(shards)),)),
             dma((max(groups - 1, 1), 2)),
-            dma((max(low - 1, 1), 2)),
-            dma((max(shards // low - 1, 1), 2)),
+            dma(()),
+            dma((shards,)),
+            dma((shards,)),
+            dma(()),
             dma((others, 2)),
             dma((others, max(groups - 1, 1), 2)),
         ],

time: 29 us -> 28.7 us (0.990)
  Pallas kernels: 28.9 us -> 28.4 us
    pallas_call x1, Pallas kernels: 27.9 us -> 27.4 us  [on_device(): pl.pallas_call(functools.partial(kernel, (layers, rows, width, tasks, sha...]
where the time goes in v2:
time: 28.7 us; the launch traced here: 28.4 us
  Pallas kernels  28.4 us (99%)
    pallas_call x1, Pallas kernels, on_device(): pl.pallas_call(functools.partial(kernel, (layers, rows, width, tasks, sha...  27.4 us
    pallas_call x1, Pallas kernels, on_device(): pl.pallas_call(put_out, out_shape=jax.ShapeDtypeStruct(result.shape, resu...  0.98 us

profile of v2, /device:TPU:0, one launch (start us, length us, event | category | flops | bytes accessed | tf_op | source)
XLA Modules:
  0.0 28.4 jit_solution(7772087410825140230)
XLA Ops:
  0.0 27.4 %merge.1.value = bf16[4,16,8192]{2,1,0:T(8,128)(2,1)S(1)} custom-call(bf16[1,4,16,16384]{3,2,1,0:T(8,128)(2,1)} %delta_hbm.1, s32[1,4,16,16384]{3,2,1,0:T(8,128)} %score_hbm.1, s32[1,4,8]{2,1,0:T(4,128)} %limit_hbm.1), custom_call_target="tpu_custom_call" | custom-call | tf_op jit(solution)/shard_map/merge/pallas_call | solution.py:361
  27.5 1.0 %put.1 = bf16[4,16,8192]{2,1,0:T(8,128)(2,1)} custom-call(bf16[4,16,8192]{2,1,0:T(8,128)(2,1)S(1)} %merge.1.value), custom_call_target="tpu_custom_call" | custom-call | tf_op jit(solution)/shard_map/put/pallas_call | solution.py:406

commit v3 on v2

--- a/solution.py
+++ b/solution.py
@@ -21,28 +21,35 @@
     unit = 128 * groups
     raw = columns // 2 // unit * unit
     first = min(1024, raw // 4 // 128 * 128)
-    last = min(1024, (columns - raw) // 2 // 128 * 128)
+    last = min(1024, (columns - raw) // 4 // 128 * 128)
     raw_units, scaled_units = [], []
-    for l in range(layers):
-        for k in range(1, tasks):
-            if l == 0 and k == 1:
-                raw_units += [(l, k, 0, first), (l, k, first, first), (l, k, 2 * first, raw - 2 * first)]
-            else:
-                raw_units.append((l, k, 0, raw))
-            if l == layers - 1:
-                cut = columns - last
-                scaled_units += [(l, k, raw, cut - raw), (l, k, cut, last)]
-            else:
-                scaled_units.append((l, k, raw, columns - raw))
+    for k in range(1, tasks):
+        if k == 1:
+            raw_units += [(k, 0, 1, 0, first), (k, 0, 1, first, first), (k, 0, 1, 2 * first, raw - 2 * first)]
+        else:
+            raw_units.append((k, 0, 1, 0, raw))
+    for k in range(1, tasks):
+        raw_units.append((k, 1, layers - 1, 0, raw))
+    for k in range(1, tasks):
+        scaled_units += [(k, 0, 1, raw, columns - raw), (k, 1, layers - 2, raw, columns - raw)]
+    for k in range(1, tasks):
+        cut = columns - last
+        scaled_units += [(k, layers - 1, 1, raw, cut - raw), (k, layers - 1, 1, cut, last)]
     return raw, raw_units, scaled_units
+
+
+def detours(columns, tasks, shards, groups):
+    if tasks != 2:
+        return [], 0
+    return [HUB + groups * j for j in range(1, 4) if HUB + groups * j < shards], columns // 16 // 128 * 128
 
 
 def kernel(
     sizes, delta_hbm, score_hbm, limit_hbm, merged,
     limit_ref, delta, score, outgoing, incoming, sums, sums_in, part, part_in, total_ref,
-    chance, chance_in, own_rate, out_rate, in_rate, own,
-    limit_sem, unit_sem, later_sem, rest_sem, send_sem, recv_sem,
-    sums_sem, part_send, part_recv, total_send, total_recv, chance_sem, share_sem,
+    chance, chance_in, own_rate, out_rate, in_rate, own, detoured,
+    limit_sem, unit_sem, rest_sem, send_sem, recv_sem,
+    sums_sem, part_send, part_recv, total_send, total_recv, chance_sem, share_sem, leg_sem,
 ):
     layers, rows, width, tasks, shards = sizes
     columns = width // tasks
@@ -98,26 +105,22 @@
         copy.start()
         return copy
 
-    every, later = pl.ds(0, layers), pl.ds(1, layers - 1)
-    unit_loads = {}
-    for u, (l, k, c, n) in enumerate(raw_units):
-        if l == 0:
-            unit_loads[u] = [
-                load(score_hbm, score, k, l, c, n, unit_sem.at[u, 0]),
-                load(delta_hbm, delta, k, l, c, n, unit_sem.at[u, 1]),
-            ]
-    later_loads = {k: load(delta_hbm, delta, k, later, 0, columns, later_sem.at[k]) for k in range(1, tasks)}
-    for u, (l, k, c, n) in enumerate(raw_units):
-        if l:
-            unit_loads[u] = [load(score_hbm, score, k, l, c, n, unit_sem.at[u, 0])]
+    unit_loads = []
+    for u, (k, l, deep, c, n) in enumerate(raw_units):
+        wide = 0 if l == 0 else columns - n
+        unit_loads.append([
+            load(score_hbm, score, k, pl.ds(l, deep), c, n, unit_sem.at[u, 0]),
+            load(delta_hbm, delta, k, pl.ds(l, deep), c, n + wide, unit_sem.at[u, 1]),
+        ])
+    every = pl.ds(0, layers)
+    ks = list(range(1, tasks)) + [0]
     delta_loads = [
-        load(delta_hbm, delta, k, 0, raw, columns - raw, rest_sem.at[0, k]) if k
-        else load(delta_hbm, delta, 0, every, 0, columns, rest_sem.at[0, 0])
-        for k in list(range(1, tasks)) + [0]
+        load(delta_hbm, delta, k, pl.ds(0, 1) if k else every, raw if k else 0, columns - (raw if k else 0), rest_sem.at[0, k])
+        for k in ks
     ]
     score_loads = {
         k: load(score_hbm, score, k, every, raw if k else 0, columns - (raw if k else 0), rest_sem.at[1, k])
-        for k in list(range(1, tasks)) + [0]
+        for k in ks
     }
 
     @pl.when(is_hub)
@@ -129,29 +132,48 @@
         limit = limit_ref[l, expert]
         return jnp.where(score[k, l, :, at] < limit, delta[k, l, :, at].astype(F32), 0.0)
 
-    sends = []
-    for u, (l, k, c, n) in enumerate(raw_units + scaled_units):
-        sends.append(pltpu.make_async_remote_copy(
-            src_ref=outgoing.at[k - 1, l, :, pl.ds(c, n)],
-            dst_ref=incoming.at[k - 1, l, :, pl.ds(c, n)],
+    def to_task(u, k, l, deep, c, n):
+        where = (k - 1, pl.ds(l, deep), slice(None), pl.ds(c, n))
+        return pltpu.make_async_remote_copy(
+            src_ref=outgoing.at[where], dst_ref=incoming.at[where],
             send_sem=send_sem.at[u], recv_sem=recv_sem.at[u],
             device_id={"task": task_peer(k)}, device_id_type=MESH,
-        ))
+        )
+
+    def to_shard(src, dst, send, recv, s, task=None):
+        where = {"shard": s} if task is None else {"shard": s, "task": task}
+        return pltpu.make_async_remote_copy(
+            src_ref=src, dst_ref=dst, send_sem=send, recv_sem=recv, device_id=where, device_id_type=MESH
+        )
+
+    sends = [to_task(u, *unit) for u, unit in enumerate(raw_units + scaled_units)]
+    split = len(raw_units) + len(scaled_units) - 2
+    helpers, detour = detours(columns, tasks, shards, groups)
+    hub_sends = jnp.logical_and(is_hub, me_task == 1)
+    hub_takes = jnp.logical_and(is_hub, me_task == 0)
+    if helpers:
+        k, l, deep, c, n = (raw_units + scaled_units)[split]
+        skipped = detour * len(helpers)
+        hub_copy = to_task(split, k, l, deep, c + skipped, n - skipped)
+        legs = []
+        for j, s in enumerate(helpers):
+            at = pl.ds(c + j * detour, detour)
+            legs.append((
+                to_shard(outgoing.at[0, l, :, at], detoured.at[j], leg_sem.at[j, 0], leg_sem.at[j, 1], s, 0),
+                to_shard(detoured.at[j], incoming.at[0, l, :, at], leg_sem.at[j, 2], leg_sem.at[j, 3], HUB),
+            ))
 
     limit_copy.wait()
     early = 2
-    for u, (l, k, c, n) in enumerate(raw_units):
-        if l and later_loads:
-            for copy in later_loads.values():
-                copy.wait()
-            later_loads = None
+    for u, (k, l, deep, c, n) in enumerate(raw_units):
         for copy in unit_loads[u]:
             copy.wait()
-
-        def prepare(at, l=l, k=k):
-            outgoing[k - 1, l, :, at] = masked(l, k, at).astype(BF16)
-
-        sweep(c, n, prepare)
+        for layer in range(l, l + deep):
+
+            def prepare(at, layer=layer, k=k):
+                outgoing[k - 1, layer, :, at] = masked(layer, k, at).astype(BF16)
+
+            sweep(c, n, prepare)
         if u == 0:
             away = jnp.where(expert == HUB // groups, 0, 1)
             pl.semaphore_wait(barrier, tasks - 1 + groups - 1 + away)
@@ -195,11 +217,6 @@
 
     pairs = [exchange(sums, sums_in.at[m - 1], sums_sem.at[m - 1], m) for m in range(1, groups)]
 
-    def to_shard(src, dst, send, recv, s):
-        return pltpu.make_async_remote_copy(
-            src_ref=src, dst_ref=dst, send_sem=send, recv_sem=recv, device_id={"shard": s}, device_id_type=MESH
-        )
-
     others = [s for s in range(shards) if s != HUB]
     to_hub = to_shard(part, part_in.at[me_shard], part_send, part_recv.at[me_shard], HUB)
     to_all = {s: to_shard(total_ref, total_ref, total_send.at[s], total_recv, s) for s in others}
@@ -208,13 +225,13 @@
     def _():
         to_hub.start()
 
+    for copy in pairs:
+        copy.wait()
     for u in range(early, len(raw_units)):
         @pl.when(late_core)
         def _(u=u):
             sends[u].start()
 
-    for copy in pairs:
-        copy.wait()
     for k in range(tasks):
 
         def join(at, k=k):
@@ -270,15 +287,27 @@
 
     for k in range(1, tasks):
         score_loads[k].wait()
-    for u, (l, k, c, n) in enumerate(scaled_units):
-
-        def rescale(at, l=l, k=k):
-            value = masked(l, k, at) * out_rate[k - 1, l : l + 1, at]
-            held = jnp.clip(value, -BF16_MAX, BF16_MAX)
-            outgoing[k - 1, l, :, at] = jnp.where(jnp.abs(value) <= F32_MAX, held, value).astype(BF16)
-
-        sweep(c, n, rescale)
-        sends[len(raw_units) + u].start()
+    for u, (k, l, deep, c, n) in enumerate(scaled_units, len(raw_units)):
+        for layer in range(l, l + deep):
+
+            def rescale(at, layer=layer, k=k):
+                value = masked(layer, k, at) * out_rate[k - 1, layer : layer + 1, at]
+                held = jnp.clip(value, -BF16_MAX, BF16_MAX)
+                outgoing[k - 1, layer, :, at] = jnp.where(jnp.abs(value) <= F32_MAX, held, value).astype(BF16)
+
+            sweep(c, n, rescale)
+        if helpers and u == split:
+            @pl.when(hub_sends)
+            def _():
+                for there, _ in legs:
+                    there.start()
+                hub_copy.start()
+
+            @pl.when(jnp.logical_not(hub_sends))
+            def _():
+                sends[split].start()
+        else:
+            sends[u].start()
 
     score_loads[0].wait()
 
@@ -309,37 +338,63 @@
 
         sweep(0, raw, invert_in)
 
-    for u, (l, k, c, n) in enumerate(raw_units):
+    def combine(k, l, deep, c, n, scaled):
+        for layer in range(l, l + deep):
+
+            def add(at, layer=layer):
+                value = incoming[k - 1, layer, :, at].astype(F32)
+                if not scaled:
+                    value = value * in_rate[k - 1, layer : layer + 1, at]
+                value = own[layer, :, at] + value
+                if k < tasks - 1:
+                    own[layer, :, at] = value
+                else:
+                    merged[layer, :, at] = value.astype(BF16)
+
+            sweep(c, n, add)
+
+    for u, unit in enumerate(raw_units):
         sends[u].wait()
-
-        def add_raw(at, l=l, k=k):
-            own[l, :, at] = own[l, :, at] + incoming[k - 1, l, :, at].astype(F32) * in_rate[k - 1, l : l + 1, at]
-
-        if k < tasks - 1:
-            sweep(c, n, add_raw)
-            continue
-
-        def end_raw(at, l=l, k=k):
-            value = own[l, :, at] + incoming[k - 1, l, :, at].astype(F32) * in_rate[k - 1, l : l + 1, at]
-            merged[l, :, at] = value.astype(BF16)
-
-        sweep(c, n, end_raw)
+        combine(*unit, scaled=False)
+
+    for j, s in enumerate(helpers):
+        @pl.when(jnp.logical_and(me_shard == s, me_task == 0))
+        def _(j=j):
+            legs[j][0].wait_recv()
+            legs[j][1].start()
 
     @pl.when(is_hub)
     def _():
         for s in others:
             to_all[s].wait_send()
 
-    for u, (l, k, c, n) in enumerate(scaled_units):
-        sends[len(raw_units) + u].wait()
-
-        def add_scaled(at, l=l, k=k):
-            own[l, :, at] = own[l, :, at] + incoming[k - 1, l, :, at].astype(F32)
-
-        def end_scaled(at, l=l, k=k):
-            merged[l, :, at] = (own[l, :, at] + incoming[k - 1, l, :, at].astype(F32)).astype(BF16)
-
-        sweep(c, n, add_scaled if k < tasks - 1 else end_scaled)
+    for u, unit in enumerate(scaled_units, len(raw_units)):
+        if helpers and u == split:
+            @pl.when(hub_takes)
+            def _():
+                for _, on in legs:
+                    on.wait_recv()
+                hub_copy.wait_recv()
+                sends[split].wait_send()
+
+            @pl.when(hub_sends)
+            def _():
+                for there, _ in legs:
+                    there.wait_send()
+                hub_copy.wait_send()
+                sends[split].wait_recv()
+
+            @pl.when(jnp.logical_not(is_hub))
+            def _():
+                sends[split].wait()
+
+            for j, s in enumerate(helpers):
+                @pl.when(jnp.logical_and(me_shard == s, me_task == 0))
+                def _(j=j):
+                    legs[j][1].wait_send()
+        else:
+            sends[u].wait()
+        combine(*unit, scaled=True)
 
 
 def put_out(value, out_hbm, sem):
@@ -355,6 +410,8 @@
     others = max(tasks - 1, 1)
     groups = shards // EXPERTS
     raw, raw_units, scaled_units = plan(layers, columns, tasks, groups)
+    helpers, detour = detours(columns, tasks, shards, groups)
+    pieces = max(len(helpers), 1)
     sent = len(raw_units) + len(scaled_units)
     dma = pltpu.SemaphoreType.DMA
     keep_limits = pltpu.with_memory_space_constraint(keep_limits, pltpu.HBM)
@@ -384,9 +441,9 @@
             pltpu.VMEM((others, layers, columns), F32),
             pltpu.VMEM((others, layers, raw), F32),
             pltpu.VMEM((layers, rows, columns), F32),
+            pltpu.VMEM((pieces, rows, max(detour, 128)), BF16),
             dma(()),
             dma((len(raw_units), 2)),
-            dma((tasks,)),
             dma((2, tasks)),
             dma((sent,)),
             dma((sent,)),
@@ -397,6 +454,7 @@
             dma(()),
             dma((others, 2)),
             dma((others, max(groups - 1, 1), 2)),
+            dma((pieces, 4)),
         ],
         compiler_params=pltpu.CompilerParams(
             collective_id=0, has_side_effects=True, vmem_limit_bytes=52 * 2**20

time: 28.7 us -> 28.2 us (0.983)
  Pallas kernels: 28.4 us -> 27.8 us
    pallas_call x1, Pallas kernels: 27.4 us -> 26.8 us  [on_device(): pl.pallas_call(functools.partial(kernel, (layers, rows, width, tasks, sha...]
where the time goes in v3:
time: 28.2 us; the launch traced here: 27.8 us
  Pallas kernels  27.8 us (99%)
    pallas_call x1, Pallas kernels, on_device(): pl.pallas_call(functools.partial(kernel, (layers, rows, width, tasks, sha...  26.8 us
    pallas_call x1, Pallas kernels, on_device(): pl.pallas_call(put_out, out_shape=jax.ShapeDtypeStruct(result.shape, resu...  0.98 us

profile of v3, /device:TPU:0, one launch (start us, length us, event | category | flops | bytes accessed | tf_op | source)
XLA Modules:
  0.0 27.8 jit_solution(11892446307286866668)
XLA Ops:
  0.0 26.8 %merge.1.value = bf16[4,16,8192]{2,1,0:T(8,128)(2,1)S(1)} custom-call(bf16[1,4,16,16384]{3,2,1,0:T(8,128)(2,1)} %delta_hbm.1, s32[1,4,16,16384]{3,2,1,0:T(8,128)} %score_hbm.1, s32[1,4,8]{2,1,0:T(4,128)} %limit_hbm.1), custom_call_target="tpu_custom_call" | custom-call | tf_op jit(solution)/shard_map/merge/pallas_call | solution.py:418
  26.8 1.0 %put.1 = bf16[4,16,8192]{2,1,0:T(8,128)(2,1)} custom-call(bf16[4,16,8192]{2,1,0:T(8,128)(2,1)S(1)} %merge.1.value), custom_call_target="tpu_custom_call" | custom-call | tf_op jit(solution)/shard_map/put/pallas_call | solution.py:464

commit v4 on v3

v4 whole, which is shorter than its diff:
```python
import functools
import jax
import jax.numpy as jnp
from jax import lax
from jax.experimental import pallas as pl
from jax.experimental.pallas import tpu as pltpu
from jax.sharding import PartitionSpec as P

EXPERTS = 8
F32 = jnp.float32
BF16 = jnp.bfloat16
MESH = pl.DeviceIdType.MESH
BF16_MAX = float(jnp.finfo(BF16).max)
F32_MAX = float(jnp.finfo(F32).max)
HUB = 1


def plan(layers, columns, tasks, groups):
    unit = 128 * groups
    raw = columns // 2 // unit * unit
    first = min(512, raw // 4 // 128 * 128)
    last = min(1024, (columns - raw) // 4 // 128 * 128)
    cut = columns - last
    ks = range(1, tasks)
    raw_units = [(1, 0, 1, 0, first), (1, 0, 1, first, first), (1, 0, 1, 2 * first, raw - 2 * first)]
    raw_units += [(k, 0, 1, 0, raw) for k in ks if k > 1]
    raw_units += [(k, 1, layers - 1, 0, raw) for k in ks]
    scaled_units = [(k, 0, 1, raw, columns - raw) for k in ks]
    scaled_units += [(k, 1, layers - 2, raw, columns - raw) for k in ks]
    scaled_units += [(k, layers - 1, 1, raw, cut - raw) for k in ks]
    scaled_units += [(k, layers - 1, 1, cut, last) for k in ks]
    return raw, first, cut, raw_units, scaled_units


def detours(columns, tasks, shards, groups):
    if tasks != 2:
        return [], 0
    return [HUB + groups * j for j in range(1, 4) if HUB + groups * j < shards], columns * 5 // 64 // 128 * 128


def kernel(
    sizes, delta_hbm, score_hbm, limit_hbm, merged,
    limit_ref, delta, score, outgoing, incoming, sums, sums_in, part, part_in, total_ref,
    chance, chance_in, own_rate, out_rate, in_rate, own, detoured,
    load_sem, send_sem, recv_sem, sums_sem, hub_sem, chance_sem, leg_sem,
):
    layers, rows, width, tasks, shards = sizes
    columns = width // tasks
    groups = shards // EXPERTS
    all_bits = shards.bit_length() - 1
    raw, first, cut, raw_units, scaled_units = plan(layers, columns, tasks, groups)
    ks = list(range(1, tasks))
    me_shard, me_task = lax.axis_index("shard"), lax.axis_index("task")
    expert = me_shard // groups
    row_total = rows * groups
    is_hub = me_shard == HUB
    not_hub = jnp.logical_not(is_hub)
    others = [s for s in range(shards) if s != HUB]
    outside = [s for s in others if s // groups != HUB // groups]
    helpers, detour = detours(columns, tasks, shards, groups)

    def flipped(mask):
        index = me_shard
        for bit in range(all_bits):
            stride = 2**bit
            if mask & stride:
                index = index + stride * (1 - 2 * lax.rem(me_shard // stride, 2))
        return index

    def task_peer(k):
        return lax.rem(me_task + k, tasks)

    def remote(src, dst, send, recv, where):
        return pltpu.make_async_remote_copy(
            src_ref=src, dst_ref=dst, send_sem=send, recv_sem=recv, device_id=where, device_id_type=MESH
        )

    def sweep(start, length, body):
        step = length
        while step > 2048:
            step //= 2
        if step % 128:
            step = 128

        def turn(i, carry):
            body(pl.ds(pl.multiple_of(start + i * step, 128), step))
            return carry

        if length == step:
            body(pl.ds(start, length))
        else:
            lax.fori_loop(0, length // step, turn, 0)

    barrier = pltpu.get_barrier_semaphore()

    def greet(where):
        pl.semaphore_signal(barrier, inc=1, device_id=where, device_id_type=MESH)

    used = []

    def load(whole, held, k, l, deep, c, n):
        there = pl.ds(pl.multiple_of(task_peer(k) * columns + c, 128), n)
        copy = pltpu.make_async_copy(
            whole.at[0, pl.ds(l, deep), :, there], held.at[k, pl.ds(l, deep), :, pl.ds(c, n)],
            load_sem.at[len(used)],
        )
        used.append(copy)
        copy.start()
        return copy

    limit_copy = pltpu.make_async_copy(limit_hbm.at[0], limit_ref, load_sem.at[0])
    used.append(limit_copy)
    limit_copy.start()
    first_loads = [load(score_hbm, score, 1, 0, 1, 0, first), load(delta_hbm, delta, 1, 0, 1, 0, first)]
    for k in ks:
        greet({"task": task_peer(k)})
    for mask in range(1, groups):
        greet({"shard": flipped(mask)})
    top_loads, deep_loads, own_loads = [], [], []
    for k in ks:
        c = first if k == 1 else 0
        top_loads.append(load(score_hbm, score, k, 0, 1, c, raw - c))
        top_loads.append(load(delta_hbm, delta, k, 0, 1, c, columns - c))
    for k in ks:
        deep_loads.append(load(score_hbm, score, k, 1, layers - 1, 0, raw))
        deep_loads.append(load(delta_hbm, delta, k, 1, layers - 1, 0, columns))
    own_loads.append(load(delta_hbm, delta, 0, 0, layers, 0, columns))
    score_loads = [load(score_hbm, score, k, 0, layers, raw, columns - raw) for k in ks]
    own_score_load = load(score_hbm, score, 0, 0, layers, 0, columns)

    @pl.when(is_hub)
    def _():
        for s in outside:
            greet({"shard": s})

    def masked(l, k, at):
        limit = limit_ref[l, expert]
        return jnp.where(score[k, l, :, at] < limit, delta[k, l, :, at].astype(F32), 0.0)

    def to_task(k, l, deep, c, n, recv):
        where = (k - 1, pl.ds(l, deep), slice(None), pl.ds(c, n))
        return remote(outgoing.at[where], incoming.at[where], send_sem, recv_sem.at[recv], {"task": task_peer(k)})

    raw_sends = [to_task(*unit, 0) for unit in raw_units]
    scaled_sends = [to_task(*unit, 1 + u // (2 * len(ks)) + u // (3 * len(ks))) for u, unit in enumerate(scaled_units)]
    hub_sends = jnp.logical_and(is_hub, me_task == 1)
    split = len(scaled_units) - 2
    legs = []
    if helpers:
        k, l, deep, c, n = scaled_units[split]
        skipped = detour * len(helpers)
        hub_copy = to_task(k, l, deep, c + skipped, n - skipped, 2)
        for j, s in enumerate(helpers):
            at = pl.ds(c + j * detour, detour)
            legs.append((
                remote(outgoing.at[0, l, :, at], detoured, send_sem, leg_sem.at[0], {"shard": s, "task": 0}),
                remote(detoured, incoming.at[0, l, :, at], leg_sem.at[1], recv_sem.at[2], {"shard": HUB}),
            ))

    limit_copy.wait()
    early = 3
    held_back = jnp.logical_and(is_hub, tasks > 1)
    for u, (k, l, deep, c, n) in enumerate(raw_units):
        if u == 0:
            ready = first_loads
        elif u == 1:
            ready = top_loads
        elif l:
            ready, deep_loads = deep_loads, []
            own_loads = own_loads
        for copy in ready:
            copy.wait()
        ready = []
        for layer in range(l, l + deep):

            def prepare(at, layer=layer, k=k):
                outgoing[k - 1, layer, :, at] = masked(layer, k, at).astype(BF16)

            sweep(c, n, prepare)
        if u == 0:
            away = jnp.where(expert == HUB // groups, 0, 1)
            pl.semaphore_wait(barrier, tasks - 1 + groups - 1 + away)
        if u < early:
            raw_sends[u].start()
        else:
            @pl.when(jnp.logical_not(held_back))
            def _(u=u):
                raw_sends[u].start()

    for copy in own_loads:
        copy.wait()
    for k in range(tasks):
        for l in range(layers):

            def add_up(at, l=l, k=k):
                size = jnp.abs(delta[k, l, :, at].astype(F32))
                sums[k, l : l + 1, at] = jnp.sum(size, axis=0, keepdims=True)

            sweep(0, columns, add_up)
    total = jnp.zeros((layers, 128), F32)
    step = min(2048, columns)
    for k in range(tasks):

        def gather(i, carry, k=k):
            block = sums[k, :, pl.ds(pl.multiple_of(i * step, 128), step)]
            for j in range(step // 128):
                carry = carry + block[:, j * 128 : (j + 1) * 128]
            return carry

        total = lax.fori_loop(0, columns // step, gather, total)
    part[...] = total

    slot = lax.rem(me_shard + (shards - 1 - HUB), shards)
    to_hub = remote(part, part_in.at[slot], hub_sem.at[0], hub_sem.at[1], {"shard": HUB})
    to_all = [remote(total_ref, total_ref, hub_sem.at[0], hub_sem.at[1], {"shard": s}) for s in others]
    all_parts = remote(
        part_in.at[pl.ds(0, shards - 1)], part_in.at[pl.ds(0, shards - 1)], hub_sem.at[0], hub_sem.at[1], {"shard": HUB}
    )

    @pl.when(not_hub)
    def _():
        to_hub.start()

    for m in range(1, groups):
        remote(sums, sums_in.at[m - 1], sums_sem.at[0], sums_sem.at[1], {"shard": flipped(m)}).start()
    if groups > 1:
        pair_wait = remote(sums_in, sums_in, sums_sem.at[0], sums_sem.at[1], {"shard": HUB})
        pair_wait.wait_send()
        pair_wait.wait_recv()

    for u in range(early, len(raw_units)):
        @pl.when(held_back)
        def _(u=u):
            raw_sends[u].start()

    for k in range(tasks):

        def join(at, k=k):
            value = sums[k, :, at]
            for m in range(groups - 1):
                value = value + sums_in[m, k, :, at]
            sums[k, :, at] = value

        sweep(0, columns, join)

    @pl.when(is_hub)
    def _():
        all_parts.wait_recv()
        value = part[...]
        for s in range(shards - 1):
            value = value + part_in[s]
        total_ref[...] = value
        for copy in to_all:
            copy.start()

    @pl.when(not_hub)
    def _():
        to_all[0].wait_recv()

    total = total_ref[...]
    grand_mean = jnp.sum(total, axis=1, keepdims=True) / (EXPERTS * row_total * width)

    def keep(k, at):
        mean = sums[k, :, at] / row_total
        return (0.2 + 0.7 * mean / (mean + grand_mean)).astype(BF16)

    segment = raw // groups
    mine = pl.ds(pl.multiple_of(lax.rem(me_shard, groups) * segment, 128), segment)
    for k in ks:

        def fill(at, k=k):
            chance[k - 1, :, at] = keep(k, at)

        sweep(0, raw, fill)

        def invert_out(at, k=k):
            out_rate[k - 1, :, at] = 1.0 / keep(k, at).astype(F32)

        sweep(raw, columns - raw, invert_out)
        remote(
            chance.at[k - 1, :, mine], chance_in.at[k - 1, :, mine], chance_sem.at[0], chance_sem.at[1],
            {"task": task_peer(k)},
        ).start()

    for copy in score_loads:
        copy.wait()
    for u, (k, l, deep, c, n) in enumerate(scaled_units):
        for layer in range(l, l + deep):

            def rescale(at, layer=layer, k=k):
                value = masked(layer, k, at) * out_rate[k - 1, layer : layer + 1, at]
                held = jnp.clip(value, -BF16_MAX, BF16_MAX)
                outgoing[k - 1, layer, :, at] = jnp.where(jnp.abs(value) <= F32_MAX, held, value).astype(BF16)

            sweep(c, n, rescale)
        if helpers and u == split:
            @pl.when(hub_sends)
            def _():
                for there, _ in legs:
                    there.start()
                hub_copy.start()

            @pl.when(jnp.logical_not(hub_sends))
            def _():
                scaled_sends[split].start()
        else:
            scaled_sends[u].start()

    own_score_load.wait()

    def invert_own(at):
        own_rate[:, at] = 1.0 / keep(0, at).astype(F32)

    sweep(0, columns, invert_own)
    for l in range(layers):

        def hold(at, l=l):
            own[l, :, at] = masked(l, 0, at) * own_rate[l : l + 1, at]

        sweep(0, columns, hold)

    if ks:
        got = chance_in.at[:, :, mine]
        remote(got, got, chance_sem.at[0], chance_sem.at[1], {"shard": HUB}).wait_recv()
        for k in ks:
            for mask in range(1, groups):
                piece = chance_in.at[k - 1, :, mine]
                remote(piece, piece, chance_sem.at[0], chance_sem.at[2], {"shard": flipped(mask)}).start()
        if groups > 1:
            shared = chance_in.at[:, :, pl.ds(0, segment * (groups - 1))]
            remote(shared, shared, chance_sem.at[0], chance_sem.at[2], {"shard": HUB}).wait_recv()
    for k in ks:

        def invert_in(at, k=k):
            in_rate[k - 1, :, at] = 1.0 / chance_in[k - 1, :, at].astype(F32)

        sweep(0, raw, invert_in)

    def arrived(recv, l, deep, c, n):
        piece = incoming.at[:, pl.ds(l, deep), :, pl.ds(c, n)]
        remote(piece, piece, send_sem, recv_sem.at[recv], {"shard": HUB}).wait_recv()

    def combine(l, deep, c, n, scaled):
        for layer in range(l, l + deep):

            def add(at, layer=layer):
                total = own[layer, :, at]
                for k in ks:
                    value = incoming[k - 1, layer, :, at].astype(F32)
                    if not scaled:
                        value = value * in_rate[k - 1, layer : layer + 1, at]
                    total = total + value
                merged[layer, :, at] = total.astype(BF16)

            sweep(c, n, add)

    arrived(0, 0, layers, 0, raw)
    combine(0, layers, 0, raw, False)

    for j, s in enumerate(helpers):
        @pl.when(jnp.logical_and(me_shard == s, me_task == 0))
        def _(j=j):
            legs[j][0].wait_recv()
            legs[j][1].start()

    arrived(1, 0, layers - 1, raw, columns - raw)
    combine(0, layers - 1, raw, columns - raw, True)
    arrived(2, layers - 1, 1, raw, cut - raw)
    combine(layers - 1, 1, raw, cut - raw, True)
    remote(chance_in, chance_in, chance_sem.at[0], chance_sem.at[1], {"shard": HUB}).wait_send()

    @pl.when(is_hub)
    def _():
        all_parts.wait_send()

    @pl.when(not_hub)
    def _():
        to_hub.wait_send()

    for j, s in enumerate(helpers):
        @pl.when(jnp.logical_and(me_shard == s, me_task == 0))
        def _(j=j):
            legs[j][1].wait_send()

    arrived(3, layers - 1, 1, cut, columns - cut)
    combine(layers - 1, 1, cut, columns - cut, True)
    remote(outgoing, outgoing, send_sem, recv_sem.at[0], {"shard": HUB}).wait_send()


def put_out(value, out_hbm, sem):
    copy = pltpu.make_async_copy(value, out_hbm, sem)
    copy.start()
    copy.wait()


def on_device(task_deltas, rank_scores, keep_limits):
    tasks, shards = lax.axis_size("task"), lax.axis_size("shard")
    _, layers, rows, width = task_deltas.shape
    columns = width // tasks
    others = tasks - 1
    groups = shards // EXPERTS
    raw, _, _, _, _ = plan(layers, columns, tasks, groups)
    _, detour = detours(columns, tasks, shards, groups)
    dma = pltpu.SemaphoreType.DMA
    keep_limits = pltpu.with_memory_space_constraint(keep_limits, pltpu.HBM)
    result = pl.pallas_call(
        functools.partial(kernel, (layers, rows, width, tasks, shards)),
        out_shape=jax.ShapeDtypeStruct((layers, rows, columns), BF16),
        in_specs=[
            pl.BlockSpec(memory_space=pltpu.HBM),
            pl.BlockSpec(memory_space=pltpu.HBM),
            pl.BlockSpec(memory_space=pltpu.HBM),
        ],
        out_specs=pl.BlockSpec(memory_space=pltpu.VMEM),
        scratch_shapes=[
            pltpu.SMEM(keep_limits.shape[1:], jnp.int32),
            pltpu.VMEM((tasks, layers, rows, columns), BF16),
            pltpu.VMEM((tasks, layers, rows, columns), jnp.int32),
            pltpu.VMEM((others, layers, rows, columns), BF16),
            pltpu.VMEM((others, layers, rows, columns), BF16),
            pltpu.VMEM((tasks, layers, columns), F32),
            pltpu.VMEM((max(groups - 1, 1), tasks, layers, columns), F32),
            pltpu.VMEM((layers, 128), F32),
            pltpu.VMEM((shards - 1, layers, 128), F32),
            pltpu.VMEM((layers, 128), F32),
            pltpu.VMEM((others, layers, raw), BF16),
            pltpu.VMEM((others, layers, raw), BF16),
            pltpu.VMEM((layers, columns), F32),
            pltpu.VMEM((others, layers, columns), F32),
            pltpu.VMEM((others, layers, raw), F32),
            pltpu.VMEM((layers, rows, columns), F32),
            pltpu.VMEM((rows, max(detour, 128)), BF16),
            dma((3 + 5 * others + 2,)),
            dma(()),
            dma((4,)),
            dma((2,)),
            dma((2,)),
            dma((3,)),
            dma((2,)),
        ],
        compiler_params=pltpu.CompilerParams(
            collective_id=0, has_side_effects=True, vmem_limit_bytes=52 * 2**20
        ),
        name="merge",
    )(task_deltas, rank_scores, keep_limits)
    return pl.pallas_call(
        put_out,
        out_shape=jax.ShapeDtypeStruct(result.shape, result.dtype),
        in_specs=[pl.BlockSpec(memory_space=pltpu.VMEM)],
        out_specs=pl.BlockSpec(memory_space=pltpu.HBM),
        scratch_shapes=[dma(())],
        compiler_params=pltpu.CompilerParams(vmem_limit_bytes=4 * 2**20),
        name="put",
    )(result)


def solution(mesh):
    return jax.shard_map(
        on_device,
        mesh=mesh,
        in_specs=(
            P("task", None, "shard", None),
            P("task", None, "shard", None),
            P("task", None, None),
        ),
        out_specs=P(None, "shard", "task"),
        check_vma=False,
    )
```

time: 28.2 us -> 27.6 us (0.979)
  Pallas kernels: 27.8 us -> 27.4 us
    pallas_call x1, Pallas kernels: 26.8 us -> 26.4 us  [on_device(): pl.pallas_call(functools.partial(kernel, (layers, rows, width, tasks, sha...]
where the time goes in v4:
time: 27.6 us; the launch traced here: 27.4 us
  Pallas kernels  27.4 us (99%)
    pallas_call x1, Pallas kernels, on_device(): pl.pallas_call(functools.partial(kernel, (layers, rows, width, tasks, sha...  26.4 us
    pallas_call x1, Pallas kernels, on_device(): pl.pallas_call(put_out, out_shape=jax.ShapeDtypeStruct(result.shape, resu...  0.98 us

profile of v4, /device:TPU:0, one launch (start us, length us, event | category | flops | bytes accessed | tf_op | source)
XLA Modules:
  0.0 27.4 jit_solution(16810158882256126770)
XLA Ops:
  0.0 26.4 %merge.1.value = bf16[4,16,8192]{2,1,0:T(8,128)(2,1)S(1)} custom-call(bf16[1,4,16,16384]{3,2,1,0:T(8,128)(2,1)} %delta_hbm.1, s32[1,4,16,16384]{3,2,1,0:T(8,128)} %score_hbm.1, s32[1,4,8]{2,1,0:T(4,128)} %limit_hbm.1), custom_call_target="tpu_custom_call" | custom-call | tf_op jit(solution)/shard_map/merge/pallas_call | solution.py:406
  26.5 1.0 %put.1 = bf16[4,16,8192]{2,1,0:T(8,128)(2,1)} custom-call(bf16[4,16,8192]{2,1,0:T(8,128)(2,1)S(1)} %merge.1.value), custom_call_target="tpu_custom_call" | custom-call | tf_op jit(solution)/shard_map/put/pallas_call | solution.py:446

commit v5 on v4

--- a/solution.py
+++ b/solution.py
@@ -98,13 +98,14 @@
 
     used = []
 
-    def load(whole, held, k, l, deep, c, n):
+    def load(whole, held, k, l, deep, c, n, again=None):
         there = pl.ds(pl.multiple_of(task_peer(k) * columns + c, 128), n)
         copy = pltpu.make_async_copy(
             whole.at[0, pl.ds(l, deep), :, there], held.at[k, pl.ds(l, deep), :, pl.ds(c, n)],
-            load_sem.at[len(used)],
+            load_sem.at[len(used) if again is None else again],
         )
-        used.append(copy)
+        if again is None:
+            used.append(copy)
         copy.start()
         return copy
 
@@ -117,16 +118,16 @@
     for mask in range(1, groups):
         greet({"shard": flipped(mask)})
     top_loads, deep_loads, own_loads = [], [], []
+    second_loads = [load(score_hbm, score, 1, 0, 1, first, first), load(delta_hbm, delta, 1, 0, 1, first, first)]
     for k in ks:
-        c = first if k == 1 else 0
+        c = 2 * first if k == 1 else 0
         top_loads.append(load(score_hbm, score, k, 0, 1, c, raw - c))
-        top_loads.append(load(delta_hbm, delta, k, 0, 1, c, columns - c))
+        top_loads.append(load(delta_hbm, delta, k, 0, 1, c, raw - c))
     for k in ks:
         deep_loads.append(load(score_hbm, score, k, 1, layers - 1, 0, raw))
         deep_loads.append(load(delta_hbm, delta, k, 1, layers - 1, 0, columns))
+    own_loads += [load(delta_hbm, delta, k, 0, 1, raw, columns - raw) for k in ks]
     own_loads.append(load(delta_hbm, delta, 0, 0, layers, 0, columns))
-    score_loads = [load(score_hbm, score, k, 0, layers, raw, columns - raw) for k in ks]
-    own_score_load = load(score_hbm, score, 0, 0, layers, 0, columns)
 
     @pl.when(is_hub)
     def _():
@@ -153,17 +154,20 @@
         for j, s in enumerate(helpers):
             at = pl.ds(c + j * detour, detour)
             legs.append((
-                remote(outgoing.at[0, l, :, at], detoured, send_sem, leg_sem.at[0], {"shard": s, "task": 0}),
-                remote(detoured, incoming.at[0, l, :, at], leg_sem.at[1], recv_sem.at[2], {"shard": HUB}),
+                remote(outgoing.at[0, l, :, at], detoured, send_sem, leg_sem, {"shard": s, "task": 0}),
+                remote(detoured, incoming.at[0, l, :, at], load_sem.at[1], recv_sem.at[2], {"shard": HUB}),
             ))
 
     limit_copy.wait()
     early = 3
     held_back = jnp.logical_and(is_hub, tasks > 1)
+    slow = jnp.logical_and(lax.rem(me_shard, 2) == 1, not_hub)
     for u, (k, l, deep, c, n) in enumerate(raw_units):
         if u == 0:
             ready = first_loads
         elif u == 1:
+            ready = second_loads
+        elif u == 2:
             ready = top_loads
         elif l:
             ready, deep_loads = deep_loads, []
@@ -180,13 +184,19 @@
         if u == 0:
             away = jnp.where(expert == HUB // groups, 0, 1)
             pl.semaphore_wait(barrier, tasks - 1 + groups - 1 + away)
-        if u < early:
+        if u < 3:
             raw_sends[u].start()
-        else:
-            @pl.when(jnp.logical_not(held_back))
+        elif u < early:
+            @pl.when(jnp.logical_not(slow))
             def _(u=u):
                 raw_sends[u].start()
-
+        else:
+            @pl.when(lax.rem(me_shard, 2) == 0)
+            def _(u=u):
+                raw_sends[u].start()
+
+    score_loads = [load(score_hbm, score, k, 0, layers, raw, columns - raw, 2 + k) for k in ks]
+    own_score_load = load(score_hbm, score, 0, 0, layers, 0, columns, 1)
     for copy in own_loads:
         copy.wait()
     for k in range(tasks):
@@ -209,12 +219,17 @@
 
         total = lax.fori_loop(0, columns // step, gather, total)
     part[...] = total
+    for u in range(3, len(raw_units)):
+        @pl.when(slow)
+        def _(u=u):
+            raw_sends[u].start()
+
 
     slot = lax.rem(me_shard + (shards - 1 - HUB), shards)
-    to_hub = remote(part, part_in.at[slot], hub_sem.at[0], hub_sem.at[1], {"shard": HUB})
-    to_all = [remote(total_ref, total_ref, hub_sem.at[0], hub_sem.at[1], {"shard": s}) for s in others]
+    to_hub = remote(part, part_in.at[slot], load_sem.at[2], hub_sem, {"shard": HUB})
+    to_all = [remote(total_ref, total_ref, load_sem.at[2], hub_sem, {"shard": s}) for s in others]
     all_parts = remote(
-        part_in.at[pl.ds(0, shards - 1)], part_in.at[pl.ds(0, shards - 1)], hub_sem.at[0], hub_sem.at[1], {"shard": HUB}
+        part_in.at[pl.ds(0, shards - 1)], part_in.at[pl.ds(0, shards - 1)], load_sem.at[2], hub_sem, {"shard": HUB}
     )
 
     @pl.when(not_hub)
@@ -222,9 +237,9 @@
         to_hub.start()
 
     for m in range(1, groups):
-        remote(sums, sums_in.at[m - 1], sums_sem.at[0], sums_sem.at[1], {"shard": flipped(m)}).start()
+        remote(sums, sums_in.at[m - 1], load_sem.at[0], sums_sem, {"shard": flipped(m)}).start()
     if groups > 1:
-        pair_wait = remote(sums_in, sums_in, sums_sem.at[0], sums_sem.at[1], {"shard": HUB})
+        pair_wait = remote(sums_in, sums_in, load_sem.at[0], sums_sem, {"shard": HUB})
         pair_wait.wait_send()
         pair_wait.wait_recv()
 
@@ -278,7 +293,7 @@
 
         sweep(raw, columns - raw, invert_out)
         remote(
-            chance.at[k - 1, :, mine], chance_in.at[k - 1, :, mine], chance_sem.at[0], chance_sem.at[1],
+            chance.at[k - 1, :, mine], chance_in.at[k - 1, :, mine], load_sem.at[0], chance_sem.at[0],
             {"task": task_peer(k)},
         ).start()
 
@@ -321,14 +336,14 @@
 
     if ks:
         got = chance_in.at[:, :, mine]
-        remote(got, got, chance_sem.at[0], chance_sem.at[1], {"shard": HUB}).wait_recv()
+        remote(got, got, load_sem.at[0], chance_sem.at[0], {"shard": HUB}).wait_recv()
         for k in ks:
             for mask in range(1, groups):
                 piece = chance_in.at[k - 1, :, mine]
-                remote(piece, piece, chance_sem.at[0], chance_sem.at[2], {"shard": flipped(mask)}).start()
+                remote(piece, piece, load_sem.at[0], chance_sem.at[1], {"shard": flipped(mask)}).start()
         if groups > 1:
             shared = chance_in.at[:, :, pl.ds(0, segment * (groups - 1))]
-            remote(shared, shared, chance_sem.at[0], chance_sem.at[2], {"shard": HUB}).wait_recv()
+            remote(shared, shared, load_sem.at[0], chance_sem.at[1], {"shard": HUB}).wait_recv()
     for k in ks:
 
         def invert_in(at, k=k):
@@ -367,7 +382,7 @@
     combine(0, layers - 1, raw, columns - raw, True)
     arrived(2, layers - 1, 1, raw, cut - raw)
     combine(layers - 1, 1, raw, cut - raw, True)
-    remote(chance_in, chance_in, chance_sem.at[0], chance_sem.at[1], {"shard": HUB}).wait_send()
+    remote(chance_in, chance_in, load_sem.at[0], chance_sem.at[0], {"shard": HUB}).wait_send()
 
     @pl.when(is_hub)
     def _():
@@ -430,13 +445,13 @@
             pltpu.VMEM((others, layers, raw), F32),
             pltpu.VMEM((layers, rows, columns), F32),
             pltpu.VMEM((rows, max(detour, 128)), BF16),
-            dma((3 + 5 * others + 2,)),
+            dma((6 + 5 * others,)),
             dma(()),
             dma((4,)),
+            dma(()),
+            dma(()),
             dma((2,)),
-            dma((2,)),
-            dma((3,)),
-            dma((2,)),
+            dma(()),
         ],
         compiler_params=pltpu.CompilerParams(
             collective_id=0, has_side_effects=True, vmem_limit_bytes=52 * 2**20

time: 27.6 us -> 27.4 us (level)
  no operation moved by 1% of the time
where the time goes in v5:
time: 27.4 us; the launch traced here: 27.3 us
  Pallas kernels  27.3 us (100%)
    pallas_call x1, Pallas kernels, on_device(): pl.pallas_call(functools.partial(kernel, (layers, rows, width, tasks, sha...  26.3 us
    pallas_call x1, Pallas kernels, on_device(): pl.pallas_call(put_out, out_shape=jax.ShapeDtypeStruct(result.shape, resu...  0.98 us

profile of v5, /device:TPU:0, one launch (start us, length us, event | category | flops | bytes accessed | tf_op | source)
XLA Modules:
  0.0 27.3 jit_solution(7056639588074685092)
XLA Ops:
  0.0 26.3 %merge.1.value = bf16[4,16,8192]{2,1,0:T(8,128)(2,1)S(1)} custom-call(bf16[1,4,16,16384]{3,2,1,0:T(8,128)(2,1)} %delta_hbm.1, s32[1,4,16,16384]{3,2,1,0:T(8,128)} %score_hbm.1, s32[1,4,8]{2,1,0:T(4,128)} %limit_hbm.1), custom_call_target="tpu_custom_call" | custom-call | tf_op jit(solution)/shard_map/merge/pallas_call | solution.py:421
  26.3 1.0 %put.1 = bf16[4,16,8192]{2,1,0:T(8,128)(2,1)} custom-call(bf16[4,16,8192]{2,1,0:T(8,128)(2,1)S(1)} %merge.1.value), custom_call_target="tpu_custom_call" | custom-call | tf_op jit(solution)/shard_map/put/pallas_call | solution.py:461

commit v6 on v5

--- a/solution.py
+++ b/solution.py
@@ -32,10 +32,12 @@
     return raw, first, cut, raw_units, scaled_units
 
 
-def detours(columns, tasks, shards, groups):
-    if tasks != 2:
+def detours(layers, columns, tasks, shards, groups):
+    helpers = list(range(HUB + groups, shards, groups)) if tasks == 2 else []
+    if not helpers:
         return [], 0
-    return [HUB + groups * j for j in range(1, 4) if HUB + groups * j < shards], columns * 5 // 64 // 128 * 128
+    room = plan(layers, columns, tasks, groups)[4][-2][4]
+    return helpers, min(columns * 3 // 64, room * 7 // 8 // len(helpers)) // 128 * 128
 
 
 def kernel(
@@ -57,7 +59,7 @@
     not_hub = jnp.logical_not(is_hub)
     others = [s for s in range(shards) if s != HUB]
     outside = [s for s in others if s // groups != HUB // groups]
-    helpers, detour = detours(columns, tasks, shards, groups)
+    helpers, detour = detours(layers, columns, tasks, shards, groups)
 
     def flipped(mask):
         index = me_shard
@@ -98,36 +100,37 @@
 
     used = []
 
-    def load(whole, held, k, l, deep, c, n, again=None):
+    def load(whole, held, k, l, deep, c, n, sem):
         there = pl.ds(pl.multiple_of(task_peer(k) * columns + c, 128), n)
         copy = pltpu.make_async_copy(
-            whole.at[0, pl.ds(l, deep), :, there], held.at[k, pl.ds(l, deep), :, pl.ds(c, n)],
-            load_sem.at[len(used) if again is None else again],
+            whole.at[0, pl.ds(l, deep), :, there], held.at[k, pl.ds(l, deep), :, pl.ds(c, n)], load_sem.at[sem]
         )
-        if again is None:
-            used.append(copy)
         copy.start()
         return copy
 
+    def load_both(k, l, deep, c, n, more=0):
+        sem = 1 + len(used)
+        load(score_hbm, score, k, l, deep, c, n, sem)
+        load(delta_hbm, delta, k, l, deep, c, n + more, sem)
+        both = pl.ds(0, n + (n + more) // 2)
+        used.append(pltpu.make_async_copy(
+            score_hbm.at[0, pl.ds(l, deep), :, both], score.at[k, pl.ds(l, deep), :, both], load_sem.at[sem]
+        ))
+        return used[-1]
+
+    first_load = load_both(1, 0, 1, 0, first)
     limit_copy = pltpu.make_async_copy(limit_hbm.at[0], limit_ref, load_sem.at[0])
-    used.append(limit_copy)
     limit_copy.start()
-    first_loads = [load(score_hbm, score, 1, 0, 1, 0, first), load(delta_hbm, delta, 1, 0, 1, 0, first)]
     for k in ks:
         greet({"task": task_peer(k)})
     for mask in range(1, groups):
         greet({"shard": flipped(mask)})
-    top_loads, deep_loads, own_loads = [], [], []
-    second_loads = [load(score_hbm, score, 1, 0, 1, first, first), load(delta_hbm, delta, 1, 0, 1, first, first)]
-    for k in ks:
-        c = 2 * first if k == 1 else 0
-        top_loads.append(load(score_hbm, score, k, 0, 1, c, raw - c))
-        top_loads.append(load(delta_hbm, delta, k, 0, 1, c, raw - c))
-    for k in ks:
-        deep_loads.append(load(score_hbm, score, k, 1, layers - 1, 0, raw))
-        deep_loads.append(load(delta_hbm, delta, k, 1, layers - 1, 0, columns))
-    own_loads += [load(delta_hbm, delta, k, 0, 1, raw, columns - raw) for k in ks]
-    own_loads.append(load(delta_hbm, delta, 0, 0, layers, 0, columns))
+    second_load = load_both(1, 0, 1, first, first)
+    top_loads = [load_both(k, 0, 1, 2 * first if k == 1 else 0, raw - (2 * first if k == 1 else 0)) for k in ks]
+    deep_loads = [load_both(k, 1, layers - 1, 0, raw, columns - raw) for k in ks]
+    own_sem = 1 + len(used)
+    rest_loads = [load(delta_hbm, delta, k, 0, 1, raw, columns - raw, own_sem + k) for k in ks]
+    own_load = load(delta_hbm, delta, 0, 0, layers, 0, columns, own_sem)
 
     @pl.when(is_hub)
     def _():
@@ -163,18 +166,17 @@
     held_back = jnp.logical_and(is_hub, tasks > 1)
     slow = jnp.logical_and(lax.rem(me_shard, 2) == 1, not_hub)
     for u, (k, l, deep, c, n) in enumerate(raw_units):
+        ready = []
         if u == 0:
-            ready = first_loads
+            ready = [first_load]
         elif u == 1:
-            ready = second_loads
+            ready = [second_load]
         elif u == 2:
             ready = top_loads
         elif l:
             ready, deep_loads = deep_loads, []
-            own_loads = own_loads
         for copy in ready:
             copy.wait()
-        ready = []
         for layer in range(l, l + deep):
 
             def prepare(at, layer=layer, k=k):
@@ -195,10 +197,11 @@
             def _(u=u):
                 raw_sends[u].start()
 
-    score_loads = [load(score_hbm, score, k, 0, layers, raw, columns - raw, 2 + k) for k in ks]
+    score_loads = [load(score_hbm, score, k, 0, layers, raw, columns - raw, 1 + k) for k in ks]
     own_score_load = load(score_hbm, score, 0, 0, layers, 0, columns, 1)
-    for copy in own_loads:
+    for copy in rest_loads:
         copy.wait()
+    own_load.wait()
     for k in range(tasks):
         for l in range(layers):
 
@@ -226,10 +229,10 @@
 
 
     slot = lax.rem(me_shard + (shards - 1 - HUB), shards)
-    to_hub = remote(part, part_in.at[slot], load_sem.at[2], hub_sem, {"shard": HUB})
-    to_all = [remote(total_ref, total_ref, load_sem.at[2], hub_sem, {"shard": s}) for s in others]
+    to_hub = remote(part, part_in.at[slot], load_sem.at[own_sem], hub_sem, {"shard": HUB})
+    to_all = [remote(total_ref, total_ref, load_sem.at[own_sem], hub_sem, {"shard": s}) for s in others]
     all_parts = remote(
-        part_in.at[pl.ds(0, shards - 1)], part_in.at[pl.ds(0, shards - 1)], load_sem.at[2], hub_sem, {"shard": HUB}
+        part_in.at[pl.ds(0, shards - 1)], part_in.at[pl.ds(0, shards - 1)], load_sem.at[own_sem], hub_sem, {"shard": HUB}
     )
 
     @pl.when(not_hub)
@@ -313,13 +316,14 @@
             def _():
                 for there, _ in legs:
                     there.start()
-                hub_copy.start()
 
             @pl.when(jnp.logical_not(hub_sends))
             def _():
                 scaled_sends[split].start()
         else:
-            scaled_sends[u].start()
+            @pl.when(jnp.logical_not(hub_sends))
+            def _(u=u):
+                scaled_sends[u].start()
 
     own_score_load.wait()
 
@@ -372,6 +376,14 @@
     arrived(0, 0, layers, 0, raw)
     combine(0, layers, 0, raw, False)
 
+    @pl.when(hub_sends)
+    def _():
+        for u, copy in enumerate(scaled_sends):
+            if helpers and u == split:
+                hub_copy.start()
+            else:
+                copy.start()
+
     for j, s in enumerate(helpers):
         @pl.when(jnp.logical_and(me_shard == s, me_task == 0))
         def _(j=j):
@@ -415,7 +427,7 @@
     others = tasks - 1
     groups = shards // EXPERTS
     raw, _, _, _, _ = plan(layers, columns, tasks, groups)
-    _, detour = detours(columns, tasks, shards, groups)
+    _, detour = detours(layers, columns, tasks, shards, groups)
     dma = pltpu.SemaphoreType.DMA
     keep_limits = pltpu.with_memory_space_constraint(keep_limits, pltpu.HBM)
     result = pl.pallas_call(
@@ -445,7 +457,7 @@
             pltpu.VMEM((others, layers, raw), F32),
             pltpu.VMEM((layers, rows, columns), F32),
             pltpu.VMEM((rows, max(detour, 128)), BF16),
-            dma((6 + 5 * others,)),
+            dma((4 + 3 * others,)),
             dma(()),
             dma((4,)),
             dma(()),

time: 27.4 us -> 27.3 us (level)
  the two profiles are of different devices: /device:TPU:0 before, /device:TPU:2 now
where the time goes in v6:
time: 27.3 us; the launch traced here: 27.1 us
  Pallas kernels  27.1 us (99%)
    pallas_call x1, Pallas kernels, on_device(): pl.pallas_call(functools.partial(kernel, (layers, rows, width, tasks, sha...  26.2 us
    pallas_call x1, Pallas kernels, on_device(): pl.pallas_call(put_out, out_shape=jax.ShapeDtypeStruct(result.shape, resu...  0.98 us

profile of v6, /device:TPU:2, one launch (start us, length us, event | category | flops | bytes accessed | tf_op | source)
XLA Modules:
  0.0 27.1 jit_solution(12269791018917893845)
XLA Ops:
  0.0 26.2 %merge.1.value = bf16[4,16,8192]{2,1,0:T(8,128)(2,1)S(1)} custom-call(bf16[1,4,16,16384]{3,2,1,0:T(8,128)(2,1)} %delta_hbm.1, s32[1,4,16,16384]{3,2,1,0:T(8,128)} %score_hbm.1, s32[1,4,8]{2,1,0:T(4,128)} %limit_hbm.1), custom_call_target="tpu_custom_call" | custom-call | tf_op jit(solution)/shard_map/merge/pallas_call | solution.py:433
  26.2 1.0 %put.1 = bf16[4,16,8192]{2,1,0:T(8,128)(2,1)} custom-call(bf16[4,16,8192]{2,1,0:T(8,128)(2,1)S(1)} %merge.1.value), custom_call_target="tpu_custom_call" | custom-call | tf_op jit(solution)/shard_map/put/pallas_call | solution.py:473

commit v7 on v6

--- a/solution.py
+++ b/solution.py
@@ -37,7 +37,8 @@
     if not helpers:
         return [], 0
     room = plan(layers, columns, tasks, groups)[4][-2][4]
-    return helpers, min(columns * 3 // 64, room * 7 // 8 // len(helpers)) // 128 * 128
+    piece = min(columns * 3 // 64, room * 7 // 8 // len(helpers)) // 128 * 128
+    return (helpers, piece) if piece else ([], 0)
 
 
 def kernel(
@@ -149,6 +150,8 @@
     scaled_sends = [to_task(*unit, 1 + u // (2 * len(ks)) + u // (3 * len(ks))) for u, unit in enumerate(scaled_units)]
     hub_sends = jnp.logical_and(is_hub, me_task == 1)
     split = len(scaled_units) - 2
+    last_core = jnp.logical_and(lax.rem(me_shard, 2) == 1, me_task == tasks - 1)
+    mid_core = jnp.logical_and(last_core, jnp.logical_not(hub_sends))
     legs = []
     if helpers:
         k, l, deep, c, n = scaled_units[split]
@@ -317,11 +320,11 @@
                 for there, _ in legs:
                     there.start()
 
-            @pl.when(jnp.logical_not(hub_sends))
+            @pl.when(jnp.logical_not(last_core))
             def _():
                 scaled_sends[split].start()
         else:
-            @pl.when(jnp.logical_not(hub_sends))
+            @pl.when(jnp.logical_not(last_core))
             def _(u=u):
                 scaled_sends[u].start()
 
@@ -337,6 +340,11 @@
             own[l, :, at] = masked(l, 0, at) * own_rate[l : l + 1, at]
 
         sweep(0, columns, hold)
+
+    @pl.when(mid_core)
+    def _():
+        for copy in scaled_sends:
+            copy.start()
 
     if ks:
         got = chance_in.at[:, :, mine]

time: 27.3 us -> 27.3 us (level)
  no operation moved by 1% of the time
where the time goes in v7:
time: 27.3 us; the launch traced here: 27.1 us
  Pallas kernels  27.1 us (99%)
    pallas_call x1, Pallas kernels, on_device(): pl.pallas_call(functools.partial(kernel, (layers, rows, width, tasks, sha...  26.2 us
    pallas_call x1, Pallas kernels, on_device(): pl.pallas_call(put_out, out_shape=jax.ShapeDtypeStruct(result.shape, resu...  0.98 us

profile of v7, /device:TPU:2, one launch (start us, length us, event | category | flops | bytes accessed | tf_op | source)
XLA Modules:
  0.0 27.1 jit_solution(4289412523149236029)
XLA Ops:
  0.0 26.2 %merge.1.value = bf16[4,16,8192]{2,1,0:T(8,128)(2,1)S(1)} custom-call(bf16[1,4,16,16384]{3,2,1,0:T(8,128)(2,1)} %delta_hbm.1, s32[1,4,16,16384]{3,2,1,0:T(8,128)} %score_hbm.1, s32[1,4,8]{2,1,0:T(4,128)} %limit_hbm.1), custom_call_target="tpu_custom_call" | custom-call | tf_op jit(solution)/shard_map/merge/pallas_call | solution.py:441
  26.2 1.0 %put.1 = bf16[4,16,8192]{2,1,0:T(8,128)(2,1)} custom-call(bf16[4,16,8192]{2,1,0:T(8,128)(2,1)S(1)} %merge.1.value), custom_call_target="tpu_custom_call" | custom-call | tf_op jit(solution)/shard_map/put/pallas_call | solution.py:481
